TPU v7x, 32 devices: a whole 2x2x4 slice. The times are simulated.
32 devices in a mesh: replica: 8 (over z, y), tensor: 4 (over x, core).
Axes of the slice: x: 2, y: 2, z: 4, core: 2. Of those that a mesh axis runs over, the one named last changes fastest.
Arguments:
- activations: bfloat16 [8192, 2048], P('replica', 'tensor'), may hold values from -0.625 to 0.625
- grad_out: bfloat16 [8192, 7168], P('replica', 'tensor'), may hold values from -6 to 6
- weight: bfloat16 [2048, 7168], P(None, 'tensor'), may hold values from -0.0625 to 0.0625
- momentum: float32 [8, 2048, 7168], P('replica', None, 'tensor'), may hold values from -6 to 6
- freq_rows: int32 [8, 32, 112], P(None, None, 'tensor'), may hold values from 0 to 63
Outputs:
- input_grad: bfloat16 [8192, 2048], P('replica', 'tensor')
- momentum_out: float32 [8, 2048, 7168], P('replica', None, 'tensor')
- update: bfloat16 [2048, 7168], P(None, 'tensor')
All inputs are finite; a program needn't handle non-finite values.
Results may differ from a plain program's by a relative error of at most 0.001.
Values may be sent and summed in bfloat16 or wider, within the bound.
No kernel may reach another device: no remote copies, remote signals or barrier semaphores. Data moves between devices by JAX's collectives and lax.ppermute only.
A program may use at most 192 MiB of HBM per device.

v0:
```python
import functools

import jax
import jax.numpy as jnp
import numpy as np
from jax import lax
from jax.experimental import pallas as pl
from jax.experimental.pallas import tpu as pltpu
from jax.sharding import PartitionSpec as P


TILE = 64
LANES = 128
STEP = 256
PER_STEP = STEP // TILE
PAD = 8

MIB = 1 << 20


decay_rate = 0.9
highest = lax.Precision.HIGHEST


def cosine_table():
    freq = jnp.arange(TILE, dtype=jnp.float32)[:, None]
    place = jnp.arange(TILE, dtype=jnp.float32)[None, :]
    values = jnp.cos(jnp.pi * (2.0 * place + 1.0) * freq / (2.0 * TILE)) * jnp.sqrt(2.0 / TILE)
    return jnp.where(freq == 0.0, values / jnp.sqrt(2.0), values)


def cosine_constant():
    freq = np.arange(TILE)[:, None]
    place = np.arange(TILE)[None, :]
    values = np.cos(np.pi * (2 * place + 1) * freq / (2 * TILE)) * np.sqrt(2 / TILE)
    return np.where(freq == 0, values / np.sqrt(2), values).astype(np.float32)


def split3(values):
    first = values.astype(jnp.bfloat16)
    rest = values - first.astype(np.float32)
    second = rest.astype(jnp.bfloat16)
    third = (rest - second.astype(np.float32)).astype(jnp.bfloat16)
    return first, second, third


def encode(values):
    largest = jnp.maximum(jnp.max(jnp.abs(values), axis=0, keepdims=True), 1e-30)
    power = jnp.ceil(jnp.log2(largest * (1.0 / 32767.0)))
    whole = jnp.clip(jnp.round(values * jnp.exp2(-power)), -32767.0, 32767.0)
    return whole, power


def decode_block(whole, power):
    return whole * jnp.exp2(power)


def block_of(ids_ref, place, per_owner):
    return (ids_ref[0] ^ place[0]) * per_owner + place[1]


def grad_kernel(pieces, places, per_owner, chained, *refs):
    refs = list(refs)
    ids_ref, chosen_ref = refs[:2]
    acts_refs, refs = refs[2 : 2 + pieces], refs[2 + pieces :]
    go_ref, mom_ref, ct_ref = refs[:3]
    refs = refs[4:] if chained else refs[3:]
    out_ref, code_ref = refs[:2]
    go_buf, acts_buf, mom_buf, g_ref, tab_ref, rows_ref, in_sem, out_sem = refs[2:]
    steps = len(places)
    _, hidden = go_buf.shape

    def rows_of(step):
        start = block_of(ids_ref, places[step], per_owner) * STEP
        return pl.ds(pl.multiple_of(start, STEP), STEP)

    go_copy = pltpu.make_async_copy(go_ref, go_buf, in_sem.at[2 * steps])
    go_copy.start()
    step = 0
    for piece in acts_refs:
        for n in range(piece.shape[1] // STEP):
            source = piece.at[:, pl.ds(n * STEP, STEP)]
            pltpu.make_async_copy(source, acts_buf.at[step], in_sem.at[step]).start()
            source = mom_ref.at[rows_of(step), :]
            pltpu.make_async_copy(source, mom_buf.at[step], in_sem.at[steps + step]).start()
            step += 1
    for k in range(TILE):
        tab_ref[k] = jnp.broadcast_to(ct_ref[:, k : k + 1], (TILE, LANES))
    left = lax.broadcasted_iota(jnp.int32, (TILE, LANES), 1) < TILE
    go_copy.wait()
    for step in range(steps):
        here = acts_buf.at[step]
        pltpu.make_async_copy(here, here, in_sem.at[step]).wait()
        g_ref[...] = lax.dot_general(
            acts_buf[step], go_buf[...], (((0,), (0,)), ((), ())), preferred_element_type=jnp.float32
        )
        here = mom_buf.at[step]
        pltpu.make_async_copy(here, here, in_sem.at[steps + step]).wait()
        block = block_of(ids_ref, places[step], per_owner)

        def tile_row(tr, carry):
            rows = pl.ds(pl.multiple_of(tr * TILE, TILE), TILE)
            tile = block * PER_STEP + tr
            for pair in range(hidden // LANES):
                lanes = pl.ds(pair * LANES, LANES)
                picked = jnp.where(
                    left,
                    tab_ref[chosen_ref[tile, 2 * pair]],
                    tab_ref[chosen_ref[tile, 2 * pair + 1]],
                )
                kept = decay_rate * mom_buf[step, rows, lanes] + g_ref[rows, lanes]
                row = jnp.sum(kept * picked, axis=0, keepdims=True)
                mom_buf[step, rows, lanes] = kept - picked * row
                rows_ref[step * PER_STEP + tr, :, lanes] = row
            return carry

        lax.fori_loop(0, PER_STEP, tile_row, 0)
        pltpu.make_async_copy(mom_buf.at[step], out_ref.at[rows_of(step), :], out_sem.at[step]).start()
    whole, power = encode(jnp.concatenate([rows_ref[n] for n in range(steps * PER_STEP)], axis=0))
    power = jnp.broadcast_to(power, (PAD, power.shape[1]))
    code_ref[...] = jnp.concatenate([whole, power], axis=0).astype(jnp.int32).astype(jnp.int16)
    for step in range(steps):
        pltpu.make_async_copy(mom_buf.at[step], out_ref.at[rows_of(step), :], out_sem.at[step]).wait()


def grad_call(places, ids, chosen, acts, grad_out, momentum, per_owner, chained):
    tokens, hidden = grad_out.shape
    features = momentum.shape[0]
    steps = len(places)
    rows = steps * PER_STEP
    anywhere = pl.BlockSpec(memory_space=pl.ANY)
    operands = [ids, chosen, *acts, grad_out, momentum, cosine_constant().T.copy()]
    far = pl.BlockSpec(memory_space=pltpu.HBM)
    in_specs = [anywhere] * (len(acts) + 1) + [far]
    in_specs.append(pl.BlockSpec((TILE, TILE), lambda i, ids, cho: (0, 0)))
    aliases = {}
    if chained is not None:
        aliases = {len(operands): 0}
        operands.append(chained)
        in_specs.append(far)
    return pl.pallas_call(
        functools.partial(grad_kernel, len(acts), places, per_owner, chained is not None),
        grid_spec=pltpu.PrefetchScalarGridSpec(
            num_scalar_prefetch=2,
            grid=(1,),
            in_specs=in_specs,
            out_specs=[far, pl.BlockSpec((rows + PAD, hidden), lambda i, ids, cho: (0, 0))],
            scratch_shapes=[
                pltpu.VMEM((tokens, hidden), grad_out.dtype),
                pltpu.VMEM((steps, tokens, STEP), grad_out.dtype),
                pltpu.VMEM((steps, STEP, hidden), jnp.float32),
                pltpu.VMEM((STEP, hidden), jnp.float32),
                pltpu.VMEM((TILE, TILE, LANES), jnp.float32),
                pltpu.VMEM((rows + PAD, 1, hidden), jnp.float32),
                pltpu.SemaphoreType.DMA((2 * steps + 1,)),
                pltpu.SemaphoreType.DMA((steps,)),
            ],
        ),
        out_shape=[
            jax.ShapeDtypeStruct((features, hidden), jnp.float32),
            jax.ShapeDtypeStruct((rows + PAD, hidden), jnp.int16),
        ],
        input_output_aliases=aliases,
        cost_estimate=pl.CostEstimate(
            flops=2 * steps * STEP * tokens * hidden,
            bytes_accessed=2 * tokens * hidden + 8 * steps * STEP * hidden,
            transcendentals=0,
        ),
        compiler_params=pltpu.CompilerParams(
            vmem_limit_bytes=50 * MIB
        ),
        name="grad_step",
    )(*operands)


def partial_kernel(masks, ids_ref, go_ref, w_ref, *refs):
    out_refs, (go_buf, w_buf, out_buf, in_sem, out_sem) = refs[: len(masks)], refs[len(masks) :]
    chunks, rows, _ = go_buf.shape
    width = w_buf.shape[1]
    copies = []
    for n, mask in enumerate(masks):
        start = pl.multiple_of((ids_ref[0] ^ mask) * width, width)
        copies.append(pltpu.make_async_copy(w_ref.at[pl.ds(start, width), :], w_buf.at[n], in_sem.at[n]))
    for n in range(chunks):
        source = go_ref.at[pl.ds(n * rows, rows), :]
        copies.append(pltpu.make_async_copy(source, go_buf.at[n], in_sem.at[len(masks) + n]))
    for n in (0, len(masks), *range(1, len(masks)), *range(len(masks) + 1, len(copies))):
        copies[n].start()
    outs = []
    for n in range(chunks):
        copies[len(masks) + n].wait()
        for m in range(len(masks)):
            if n == 0:
                copies[m].wait()
            out_buf[m, n] = lax.dot_general(
                go_buf[n], w_buf[m], (((1,), (1,)), ((), ())), preferred_element_type=jnp.float32
            )
            target = out_refs[m].at[pl.ds(n * rows, rows), :]
            outs.append(pltpu.make_async_copy(out_buf.at[m, n], target, out_sem.at[m, n]))
            outs[-1].start()
    for copy in outs:
        copy.wait()


def partial_call(masks, ids, grad_out, weight, width):
    tokens, hidden = grad_out.shape
    chunks = 2
    rows = tokens // chunks
    shape = jax.ShapeDtypeStruct((tokens, width), jnp.float32)
    anywhere = pl.BlockSpec(memory_space=pl.ANY)
    return pl.pallas_call(
        functools.partial(partial_kernel, masks),
        grid_spec=pltpu.PrefetchScalarGridSpec(
            num_scalar_prefetch=1,
            grid=(1,),
            in_specs=[anywhere, pl.BlockSpec(memory_space=pltpu.HBM)],
            out_specs=[anywhere] * len(masks),
            scratch_shapes=[
                pltpu.VMEM((chunks, rows, hidden), grad_out.dtype),
                pltpu.VMEM((len(masks), width, hidden), weight.dtype),
                pltpu.VMEM((len(masks), chunks, rows, width), jnp.float32),
                pltpu.SemaphoreType.DMA((len(masks) + chunks,)),
                pltpu.SemaphoreType.DMA((len(masks), chunks)),
            ],
        ),
        out_shape=[shape] * len(masks),
        cost_estimate=pl.CostEstimate(
            flops=2 * len(masks) * tokens * width * hidden,
            bytes_accessed=2 * tokens * hidden + len(masks) * width * (2 * hidden + 4 * tokens),
            transcendentals=0,
        ),
        compiler_params=pltpu.CompilerParams(
            vmem_limit_bytes=57 * MIB
        ),
        name="partial_products",
    )(ids, grad_out, weight)


def add_encode_kernel(a_ref, b_ref, out_ref):
    whole, power = encode(a_ref[...] + b_ref[...])
    power = jnp.broadcast_to(power, (2 * PAD, power.shape[1]))
    rows = whole.shape[0]
    out_ref[:rows, :] = whole.astype(jnp.int32).astype(jnp.int16)
    out_ref[rows:, :] = power.astype(jnp.int32).astype(jnp.int16)


def add_encode(a, b, blocks):
    tokens, width = a.shape
    rows = tokens // blocks
    spec = pl.BlockSpec((rows, width), lambda i: (i, 0))
    return pl.pallas_call(
        add_encode_kernel,
        grid=(blocks,),
        in_specs=[spec, spec],
        out_specs=pl.BlockSpec((rows + 2 * PAD, width), lambda i: (i, 0)),
        out_shape=jax.ShapeDtypeStruct((blocks * (rows + 2 * PAD), width), jnp.int16),
        cost_estimate=pl.CostEstimate(flops=8 * a.size, bytes_accessed=10 * a.size, transcendentals=0),
        compiler_params=pltpu.CompilerParams(vmem_limit_bytes=2 * MIB + 24 * rows * width),
        name="add_encode",
    )(a, b)


def add_decode_kernel(a_ref, b_ref, code_ref, out_ref):
    rows = a_ref.shape[0]
    whole = code_ref[:rows, :].astype(jnp.int32).astype(jnp.float32)
    power = code_ref[rows:, :].astype(jnp.int32).astype(jnp.float32)[:1]
    out_ref[...] = (a_ref[...] + b_ref[...] + decode_block(whole, power)).astype(out_ref.dtype)


def add_decode(a, b, code, blocks):
    tokens, width = a.shape
    rows = tokens // blocks
    spec = pl.BlockSpec((rows, width), lambda i: (i, 0))
    return pl.pallas_call(
        add_decode_kernel,
        grid=(blocks,),
        in_specs=[spec, spec, pl.BlockSpec((rows + 2 * PAD, width), lambda i: (i, 0))],
        out_specs=spec,
        out_shape=jax.ShapeDtypeStruct((tokens, width), jnp.bfloat16),
        cost_estimate=pl.CostEstimate(flops=8 * a.size, bytes_accessed=12 * a.size, transcendentals=0),
        compiler_params=pltpu.CompilerParams(vmem_limit_bytes=2 * MIB + 28 * rows * width),
        name="add_decode",
    )(a, b, code)


def update_kernel(places, per_owner, chained, ids_ref, near_ref, far_ref, freq_ref, ct_ref, *refs):
    if chained:
        refs = refs[1:]
    out_ref, held_ref, out_buf, out_sem = refs
    steps = len(places)
    rows = steps * PER_STEP
    hidden = out_ref.shape[1]
    total = near_ref.shape[0]
    replicas = 2 * total
    for side, ref in enumerate((near_ref, far_ref)):
        for slot in range(total):
            code = ref[slot].astype(jnp.int32).astype(jnp.float32)
            values = decode_block(code[:rows], code[rows : rows + 1])
            start = pl.multiple_of((ids_ref[1] ^ (2 * slot + side)) * rows, 8)
            for strip in range(hidden // LANES):
                held_ref[strip, pl.ds(start, rows), :] = values[:, strip * LANES : (strip + 1) * LANES]

    groups = hidden // (4 * TILE)
    wide = groups * LANES
    number = lax.broadcasted_iota(jnp.int32, (TILE, wide), 0)
    main = (lax.broadcasted_iota(jnp.int32, (TILE, wide), 1) % LANES) < TILE
    lane_tile = lax.broadcasted_iota(jnp.int32, (replicas, 4 * TILE), 1) // TILE

    for step in range(steps):
        block = block_of(ids_ref, places[step], per_owner)

        def tile_row(tr, carry):
            onehot = number == freq_ref[pl.ds(block * PER_STEP + tr, 1), :]
            onehot = onehot.astype(jnp.float32).astype(jnp.bfloat16)
            columns = jnp.dot(
                ct_ref[...],
                jnp.concatenate([onehot] * 3, axis=0),
                preferred_element_type=jnp.float32,
            )
            high = columns.astype(jnp.bfloat16).astype(jnp.float32)
            lhs = jnp.where(main, high, columns - high).astype(jnp.bfloat16)
            here = step * PER_STEP + tr
            row0 = pl.ds(pl.multiple_of(tr * TILE, TILE), TILE)
            for group in range(groups):
                values = jnp.concatenate(
                    [held_ref[2 * group + n, pl.ds(here, replicas, stride=rows), :] for n in range(2)],
                    axis=1,
                )
                top = values.astype(jnp.bfloat16).astype(jnp.float32)
                low = values - top
                parts = [jnp.where(lane_tile == c, part, 0.0) for part in (top, low) for c in range(4)]
                rhs = jnp.concatenate(parts, axis=0).astype(jnp.bfloat16)
                rhs = jnp.concatenate([rhs, rhs], axis=0)
                product = jnp.dot(
                    lhs[:, group * LANES : (group + 1) * LANES], rhs, preferred_element_type=jnp.float32
                )
                lanes = pl.ds(group * 4 * TILE, 4 * TILE)
                out_buf[step, row0, lanes] = product.astype(out_buf.dtype)
            return carry

        lax.fori_loop(0, PER_STEP, tile_row, 0, unroll=True)
        target = out_ref.at[pl.ds(pl.multiple_of(block * STEP, STEP), STEP), :]
        pltpu.make_async_copy(out_buf.at[step], target, out_sem.at[step]).start()
    for step in range(steps):
        block = block_of(ids_ref, places[step], per_owner)
        target = out_ref.at[pl.ds(pl.multiple_of(block * STEP, STEP), STEP), :]
        pltpu.make_async_copy(out_buf.at[step], target, out_sem.at[step]).wait()


def update_call(places, ids, near, far, freq_lanes, features, per_owner, chained):
    hidden = near.shape[2]
    steps = len(places)
    rows = steps * PER_STEP
    anywhere = pl.BlockSpec(memory_space=pltpu.HBM)
    table = jnp.concatenate(split3(cosine_constant().T), axis=1)
    operands = [ids, near, far, freq_lanes, table]
    in_specs = [
        pl.BlockSpec(near.shape, lambda i, ids: (0, 0, 0)),
        pl.BlockSpec(far.shape, lambda i, ids: (0, 0, 0)),
        pl.BlockSpec(freq_lanes.shape, lambda i, ids: (0, 0)),
        pl.BlockSpec(table.shape, lambda i, ids: (0, 0)),
    ]
    aliases = {}
    if chained is not None:
        aliases = {len(operands): 0}
        operands.append(chained)
        in_specs.append(anywhere)
    replicas = 2 * near.shape[0]
    return pl.pallas_call(
        functools.partial(update_kernel, places, per_owner, chained is not None),
        grid_spec=pltpu.PrefetchScalarGridSpec(
            num_scalar_prefetch=1,
            grid=(1,),
            in_specs=in_specs,
            out_specs=anywhere,
            scratch_shapes=[
                pltpu.VMEM((hidden // LANES, (replicas + 1) * rows, LANES), jnp.float32),
                pltpu.VMEM((steps, STEP, hidden), jnp.bfloat16),
                pltpu.SemaphoreType.DMA((steps,)),
            ],
        ),
        out_shape=jax.ShapeDtypeStruct((features, hidden), jnp.bfloat16),
        input_output_aliases=aliases,
        cost_estimate=pl.CostEstimate(
            flops=2 * rows * TILE * 512 * hidden, bytes_accessed=2 * rows * TILE * hidden, transcendentals=0
        ),
        compiler_params=pltpu.CompilerParams(
            vmem_limit_bytes=4 * MIB + 2 * rows * TILE * hidden + 4 * (replicas + 1) * rows * hidden + 4 * near.size * 4
        ),
        name="update_rows",
    )(*operands)


def flip(x, axis, mask):
    size = lax.axis_size(axis)
    return lax.ppermute(x, axis, [(i, i ^ mask) for i in range(size)])


def fast_body(activations, grad_out, weight, momentum, freq_rows):
    return fast_layer(activations, grad_out, weight, momentum, freq_rows)


def fast_layer(activations, grad_out, weight, momentum, freq_rows):
    device = lax.axis_index("tensor")
    replica = lax.axis_index("replica")
    ids = jnp.stack([device, replica])
    features, _ = weight.shape
    width = activations.shape[1]
    per_owner = width // STEP
    tile_rows, tile_cols = freq_rows.shape[1:]
    replicas = freq_rows.shape[0]

    chunks = [activations[:, n * STEP : (n + 1) * STEP] for n in range(per_owner)]
    twin = flip(activations, "tensor", 1)
    across = [flip(chunk, "tensor", 2) for chunk in chunks]
    across_twin = [flip(chunk, "tensor", 1) for chunk in across]

    for_twin, for_far = partial_call((3, 2), ids, grad_out, weight, width)
    received = flip(for_twin, "tensor", 1)
    code = add_encode(for_far, received, 2)
    code = flip(code, "tensor", 2)
    for_twin, own = partial_call((1, 0), ids, grad_out, weight, width)
    own_twin = flip(for_twin, "tensor", 1)

    chosen = lax.dynamic_index_in_dim(freq_rows, replica, 0, keepdims=False)
    kept = momentum[0]
    places = [
        tuple((mask, n) for mask in (0, 1) for n in range(per_owner)) + ((2, 0), (3, 0)),
    ] + [((2, n), (3, n)) for n in range(1, per_owner)]
    out = None
    codes = []
    for n in range(per_owner):
        acts = [across[n], across_twin[n]]
        if n == 0:
            acts = [activations, twin] + acts
        out, coded = grad_call(places[n], ids, chosen, acts, grad_out, kept, per_owner, out)
        codes.append(coded)

    lanes = freq_rows.reshape(replicas, tile_rows, tile_cols // 4, 1, 4)
    lanes = jnp.transpose(lanes, (1, 2, 3, 4, 0))
    lanes = jnp.broadcast_to(lanes, (tile_rows, tile_cols // 4, 4, 4, replicas))
    lanes = lanes.reshape(tile_rows, tile_cols // 4 * 16 * replicas)
    lanes = jnp.pad(lanes, ((0, PAD), (0, 0)))
    update = None
    for n in range(per_owner):
        near = jnp.stack([codes[n]] + [flip(codes[n], "replica", mask) for mask in range(2, replicas, 2)])
        far = flip(near, "replica", 1)
        update = update_call(places[n], ids, near, far, lanes, features, per_owner, update)

    input_grad = add_decode(own, own_twin, code, 2)
    return (input_grad, out[None], update)


def decode(coeff_all, chosen_all, basis):
    onehot = (chosen_all[..., None] == jnp.arange(TILE, dtype=jnp.int32)).astype(jnp.float32)
    summed = jnp.einsum("rack,racj->ackj", onehot, coeff_all, precision=highest)
    right_done = jnp.einsum("ackj,jm->ackm", summed, basis, precision=highest)
    decoded = jnp.einsum("kn,ackm->ancm", basis, right_done, precision=highest)
    return decoded.reshape(summed.shape[0] * TILE, summed.shape[1] * TILE)


def any_body(activations, grad_out, weight, momentum, freq_rows):
    basis = cosine_table()
    partial_value = lax.dot_general(
        grad_out, weight, (((1,), (1,)), ((), ())), preferred_element_type=jnp.float32
    )
    input_grad = lax.psum_scatter(partial_value, "tensor", scatter_dimension=1, tiled=True).astype(
        jnp.bfloat16
    )
    weight_grad = lax.dot_general(
        lax.all_gather(activations, "tensor", axis=1, tiled=True),
        grad_out,
        (((0,), (0,)), ((), ())),
        preferred_element_type=jnp.float32,
    )
    feature_count = weight_grad.shape[0]
    hidden_count = weight_grad.shape[1]
    tile_rows = feature_count // TILE
    tile_cols = hidden_count // TILE
    kept = decay_rate * momentum[0] + weight_grad
    my_index = lax.axis_index("replica")
    chosen = lax.dynamic_index_in_dim(freq_rows, my_index, 0, keepdims=False)
    tile_view = kept.reshape(tile_rows, TILE, tile_cols, TILE)
    half_done = jnp.einsum("ancm,lm->ancl", tile_view, basis, precision=highest)
    onehot = (chosen[:, :, None] == jnp.arange(TILE, dtype=jnp.int32)[None, None, :]).astype(
        jnp.float32
    )
    picked = jnp.einsum("ack,kn->acn", onehot, basis, precision=highest)
    coeff_rows = jnp.einsum("acn,ancl->acl", picked, half_done, precision=highest)
    spread = jnp.einsum("acj,jm->acm", coeff_rows, basis, precision=highest)
    removed = jnp.einsum("acn,acm->ancm", picked, spread)
    momentum_out = (kept - removed.reshape(feature_count, hidden_count))[None]
    share = tile_rows // lax.axis_size("replica")
    received = lax.all_to_all(coeff_rows[None], "replica", split_axis=1, concat_axis=0, tiled=True)
    mine_chosen = lax.dynamic_slice_in_dim(freq_rows, my_index * share, share, 1)
    band_update = decode(received, mine_chosen, basis).astype(jnp.bfloat16)
    update = lax.all_gather(band_update, "replica", axis=0, tiled=True)
    return (input_grad, momentum_out, update)


def fits(sizes, tokens, width, hidden):
    return (
        sizes["tensor"] == 4
        and sizes["replica"] == 8
        and tokens % 32 == 0
        and width == 2 * STEP
        and hidden % (4 * TILE) == 0
    )


def body(activations, grad_out, weight, momentum, freq_rows):
    sizes = {axis: lax.axis_size(axis) for axis in ("replica", "tensor")}
    fast = fits(sizes, *activations.shape, weight.shape[1])
    return (fast_body if fast else any_body)(activations, grad_out, weight, momentum, freq_rows)


def solution(mesh):
    placed = (
        P("replica", "tensor"),
        P("replica", "tensor"),
        P(None, "tensor"),
        P("replica", None, "tensor"),
        P(None, None, "tensor"),
    )
    return jax.shard_map(
        body,
        mesh=mesh,
        in_specs=placed,
        out_specs=(P("replica", "tensor"), P("replica", None, "tensor"), P(None, "tensor")),
        check_vma=False,
    )
```

profile of v0, /device:TPU:0, one launch (start us, length us, event | category | flops | bytes accessed | tf_op | source)
XLA Modules:
  0.0 100.1 jit_solution(10056415789077338226)
XLA Ops:
  0.6 0.7 pad_add_fusion.2.ids_ref.refs_0_
  1.3 8.3 %partial_products.3 = (f32[1024,512]{1,0:T(8,128)}, f32[1024,512]{1,0:T(8,128)}) custom-call(s32[2]{0:T(128)} %pad_add_fusion.2.ids_ref.refs_0_, bf16[1024,1792]{1,0:T(8,128)(2,1)} %refs_4_.1, bf16[2048,1792]{1,0:T(8,128)(2,1)} %w_ref.3), custom_call_target="tpu_custom_call" | custom-call | flops 3758096384 | bytes 11534336 | tf_op jit(solution)/shard_map/partial_products/pallas_call | solution.py:211
  9.6 0.6 collective-permute-start.1
  10.1 0.0 copy-done
  10.1 0.9 fusion
  11.0 2.5 %collective-permute-start.6 = (bf16[1024,256]{1,0:T(8,128)(2,1)S(1)}, bf16[1024,256]{1,0:T(8,128)(2,1)}, u32[]{:S(2)}, u32[]{:S(2)}) collective-permute-start(bf16[1024,256]{1,0:T(8,128)(2,1)S(1)} %get-tuple-element.19), channel_id=1, source_target_pairs={{0,2},{1,3},{2,0},{3,1},{4,6},{5,7},{6,4},{7,5},{8,10},{9,11},{10,... | collective-permute-start | bytes 1572872 | tf_op jit(solution)/shard_map/ppermute | solution.py:396
  13.5 0.2 collective-permute-start.5
  13.7 0.3 collective-permute-start.3
  14.0 12.4 %collective-permute-done.6.refs_4_ = bf16[1024,256]{1,0:T(8,128)(2,1)} collective-permute-done((bf16[1024,256]{1,0:T(8,128)(2,1)S(1)}, bf16[1024,256]{1,0:T(8,128)(2,1)}, u32[]{:S(2)}, u32[]{:S(2)}) %collective-permute-start.6) | collective-permute-done | bytes 524320 | tf_op jit(solution)/shard_map/ppermute | solution.py:396
  26.4 0.0 collective-permute-start.7
  26.4 8.1 %partial_products.2 = (f32[1024,512]{1,0:T(8,128)}, f32[1024,512]{1,0:T(8,128)}) custom-call(s32[2]{0:T(128)} %pad_add_fusion.2.ids_ref.refs_0_, bf16[1024,1792]{1,0:T(8,128)(2,1)} %refs_4_.1, bf16[2048,1792]{1,0:T(8,128)(2,1)} %w_ref.3), custom_call_target="tpu_custom_call" | custom-call | flops 3758096384 | bytes 11534336 | tf_op jit(solution)/shard_map/partial_products/pallas_call | solution.py:211
  34.5 0.6 collective-permute-start
  35.1 0.0 copy-done.6
  35.1 0.1 copy.20
  35.2 2.2 %collective-permute-done.3.refs_2_ = bf16[1024,256]{1,0:T(8,128)(2,1)} collective-permute-done((bf16[1024,256]{1,0:T(8,128)(2,1)}, bf16[1024,256]{1,0:T(8,128)(2,1)}, u32[]{:S(2)}, u32[]{:S(2)}) %collective-permute-start.3) | collective-permute-done | bytes 524320 | tf_op jit(solution)/shard_map/ppermute | solution.py:396
  37.4 0.0 collective-permute-start.4
  37.4 0.0 collective-permute-done.5.refs_3_
  37.4 0.0 collective-permute-done.7.refs_5_
  37.4 15.5 %grad_step.2 = (f32[2048,1792]{1,0:T(8,128)}, s16[32,1792]{1,0:T(8,128)(2,1)S(1)}) custom-call(s32[2]{0:T(128)S(1)} %copy-done.5, s32[32,28]{1,0:T(8,128)S(1)} %bitcast.19, bf16[1024,512]{1,0:T(8,128)(2,1)S(1)} %copy-done, bf16[1024,512]{1,0:T(8,128)(2,1)} %collective-permute-done.5.refs_3_, bf16[1024,256]{1,0:T(8,128)(2,1)} %collective-permute-done.6.refs_4_, ...), custom_call_target="tpu_custom_call" | custom-call | flops 5637144576 | bytes 25690112 | tf_op jit(solution)/shard_map/grad_step/pallas_call | solution.py:141
  52.9 3.9 %collective-permute-start.14 = (s16[32,1792]{1,0:T(8,128)(2,1)S(1)}, s16[32,1792]{1,0:T(8,128)(2,1)S(1)}, u32[]{:S(2)}, u32[]{:S(2)}) collective-permute-start(s16[32,1792]{1,0:T(8,128)(2,1)S(1)} %get-tuple-element.18), channel_id=1, source_target_pairs={{0,24},{4,28},{8,16},{12,20},{16,8},{20,12},{24,0},{28,4},{1,25},{... | collective-permute-start | bytes 344072 | tf_op jit(solution)/shard_map/ppermute | solution.py:396
  56.8 0.0 collective-permute-start.13
  56.9 0.0 collective-permute-done.1.b_ref
  56.9 0.6 collective-permute-start.12
  57.5 2.8 %add_encode.1 = s16[1056,512]{1,0:T(8,128)(2,1)} custom-call(f32[1024,512]{1,0:T(8,128)S(1)} %copy-done.2, f32[1024,512]{1,0:T(8,128)} %collective-permute-done.1.b_ref), custom_call_target="tpu_custom_call" | custom-call | flops 4194304 | bytes 5242880 | tf_op jit(solution)/shard_map/add_encode/pallas_call | solution.py:251
  60.3 0.6 collective-permute-done.14
  61.0 1.7 %collective-permute-start.2 = (s16[1056,512]{1,0:T(8,128)(2,1)}, s16[1056,512]{1,0:T(8,128)(2,1)}, u32[]{:S(2)}, u32[]{:S(2)}) collective-permute-start(s16[1056,512]{1,0:T(8,128)(2,1)} %add_encode.1), channel_id=1, source_target_pairs={{0,2},{1,3},{2,0},{3,1},{4,6},{5,7},{6,4},{7,5},{8,10},{9,11},{10,... | collective-permute-start | bytes 3244040 | tf_op jit(solution)/shard_map/ppermute | solution.py:396
  62.7 4.5 %collective-permute-done.13 = s16[32,1792]{1,0:T(8,128)(2,1)S(1)} collective-permute-done((s16[32,1792]{1,0:T(8,128)(2,1)S(1)}, s16[32,1792]{1,0:T(8,128)(2,1)S(1)}, u32[]{:S(2)}, u32[]{:S(2)}) %collective-permute-start.13) | collective-permute-done | bytes 114720 | tf_op jit(solution)/shard_map/ppermute | solution.py:396
  67.2 0.0 collective-permute-done.12
  67.2 1.6 %collective-permute-start.15 = (s16[4,32,1792]{2,1,0:T(8,128)(2,1)S(1)}, s16[4,32,1792]{2,1,0:T(8,128)(2,1)S(1)}, u32[]{:S(2)}, u32[]{:S(2)}) collective-permute-start(s16[4,32,1792]{2,1,0:T(8,128)(2,1)S(1)} %pad_add_fusion.near_ref), channel_id=1, source_target_pairs={{0,4},{4,0},{8,12},{12,8},{16,20},{20,16},{24,28},{28,24},{1,5},{5... | collective-permute-start | bytes 1376264 | tf_op jit(solution)/shard_map/ppermute | solution.py:396
  68.8 0.0 collective-permute-done.4.refs_3_
  68.8 8.2 %grad_step.3 = (f32[2048,1792]{1,0:T(8,128)}, s16[16,1792]{1,0:T(8,128)(2,1)S(1)}) custom-call(s32[2]{0:T(128)S(1)} %copy-done.5, s32[32,28]{1,0:T(8,128)S(1)} %bitcast.20, bf16[1024,256]{1,0:T(8,128)(2,1)} %collective-permute-done.3.refs_2_, bf16[1024,256]{1,0:T(8,128)(2,1)S(1)} %collective-permute-done.4.refs_3_, ...), custom_call_target="tpu_custom_call", output_to_operand_aliasing={{0}: (7, {})} | custom-call | flops 1879048192 | bytes 11010048 | tf_op jit(solution)/shard_map/grad_step/pallas_call | solution.py:141
  77.0 2.6 %collective-permute-start.10 = (s16[16,1792]{1,0:T(8,128)(2,1)S(1)}, s16[16,1792]{1,0:T(8,128)(2,1)S(1)}, u32[]{:S(2)}, u32[]{:S(2)}) collective-permute-start(s16[16,1792]{1,0:T(8,128)(2,1)S(1)} %get-tuple-element.17), channel_id=1, source_target_pairs={{0,24},{4,28},{8,16},{12,20},{16,8},{20,12},{24,0},{28,4},{1,25},{... | collective-permute-start | bytes 172040 | tf_op jit(solution)/shard_map/ppermute | solution.py:396
  79.6 0.0 collective-permute-start.9
  79.6 3.5 %collective-permute-done.10 = s16[16,1792]{1,0:T(8,128)(2,1)S(1)} collective-permute-done((s16[16,1792]{1,0:T(8,128)(2,1)S(1)}, s16[16,1792]{1,0:T(8,128)(2,1)S(1)}, u32[]{:S(2)}, u32[]{:S(2)}) %collective-permute-start.10) | collective-permute-done | bytes 57376 | tf_op jit(solution)/shard_map/ppermute | solution.py:396
  83.0 0.0 collective-permute-start.8
  83.0 0.8 broadcast_in_dim.12
  83.9 1.2 %copy.21 = s32[32,896]{1,0:T(8,128)S(1)} copy(s32[32,896]{0,1:T(8,128)} %bitcast.26) | data formatting | bytes 229376 | tf_op jit(solution)/shard_map/reshape | solution.py:442
  85.1 0.0 collective-permute-done.9
  85.1 2.1 %collective-permute-done.8 = s16[16,1792]{1,0:T(8,128)(2,1)S(1)} collective-permute-done((s16[16,1792]{1,0:T(8,128)(2,1)S(1)}, s16[16,1792]{1,0:T(8,128)(2,1)S(1)}, u32[]{:S(2)}, u32[]{:S(2)}) %collective-permute-start.8) | collective-permute-done | bytes 57376 | tf_op jit(solution)/shard_map/ppermute | solution.py:396
  87.2 0.6 collective-permute-start.11
  87.8 0.0 collective-permute-done.15.far_ref
  87.8 6.7 %update_rows.2.refs_0_ = bf16[2048,1792]{1,0:T(8,128)(2,1)} custom-call(s32[2]{0:T(128)S(1)} %copy-done.5, s16[4,32,1792]{2,1,0:T(8,128)(2,1)S(1)} %pad_add_fusion.near_ref, s16[4,32,1792]{2,1,0:T(8,128)(2,1)S(1)} %collective-permute-done.15.far_ref, s32[40,896]{1,0:T(8,128)S(1)} %pad.4.freq_ref, bf16[64,192]{1,0:T(8,128)(2,1)S(1)} %copy-done.4), custom_call_target="tpu_custom_call" | custom-call | flops 2818572288 | bytes 5505024 | tf_op jit(solution)/shard_map/update_rows/pallas_call | solution.py:369
  94.5 0.0 copy-start.1
  94.5 0.0 collective-permute-done.11.far_ref
  94.5 3.3 %update_rows.3 = bf16[2048,1792]{1,0:T(8,128)(2,1)} custom-call(s32[2]{0:T(128)S(1)} %copy-done.5, s16[4,16,1792]{2,1,0:T(8,128)(2,1)S(1)} %pad_add_fusion.1.near_ref, s16[4,16,1792]{2,1,0:T(8,128)(2,1)S(1)} %collective-permute-done.11.far_ref, s32[40,896]{1,0:T(8,128)S(1)} %pad.4.freq_ref, ...), custom_call_target="tpu_custom_call", output_to_operand_aliasing={{}: (5, {})} | custom-call | flops 939524096 | bytes 1835008 | tf_op jit(solution)/shard_map/update_rows/pallas_call | solution.py:369
  97.8 0.0 collective-permute-done.b_ref
  97.8 0.0 collective-permute-done.2.code_ref
  97.8 2.3 %add_decode.1 = bf16[1024,512]{1,0:T(8,128)(2,1)} custom-call(f32[1024,512]{1,0:T(8,128)S(1)} %copy-done.1, f32[1024,512]{1,0:T(8,128)S(1)} %collective-permute-done.b_ref, s16[1056,512]{1,0:T(8,128)(2,1)} %collective-permute-done.2.code_ref), custom_call_target="tpu_custom_call" | custom-call | flops 4194304 | bytes 6291456 | tf_op jit(solution)/shard_map/add_decode/pallas_call | solution.py:274
  (15 shorter events, 0.1 us)
Async XLA Ops:
  1.3 8.8 %copy-start = (bf16[1024,512]{1,0:T(8,128)(2,1)S(1)}, bf16[1024,512]{1,0:T(8,128)(2,1)}, u32[]{:S(2)}) copy-start(bf16[1024,512]{1,0:T(8,128)(2,1)} %refs_2_.1) | copy-start | bytes 3145732
  9.6 47.3 %collective-permute-start.1 = (f32[1024,512]{1,0:T(8,128)}, f32[1024,512]{1,0:T(8,128)}, u32[]{:S(2)}, u32[]{:S(2)}) collective-permute-start(f32[1024,512]{1,0:T(8,128)} %get-tuple-element.14), channel_id=1, source_target_pairs={{0,1},{1,0},{2,3},{3,2},{4,5},{5,4},{6,7},{7,6},{8,9},{9,8},{10,11... | collective-permute-start | bytes 6291464 | tf_op jit(solution)/shard_map/ppermute | solution.py:396
  11.0 15.4 %collective-permute-start.6 = (bf16[1024,256]{1,0:T(8,128)(2,1)S(1)}, bf16[1024,256]{1,0:T(8,128)(2,1)}, u32[]{:S(2)}, u32[]{:S(2)}) collective-permute-start(bf16[1024,256]{1,0:T(8,128)(2,1)S(1)} %get-tuple-element.19), channel_id=1, source_target_pairs={{0,2},{1,3},{2,0},{3,1},{4,6},{5,7},{6,4},{7,5},{8,10},{9,11},{10,... | collective-permute-start | bytes 1572872 | tf_op jit(solution)/shard_map/ppermute | solution.py:396
  13.5 23.9 %collective-permute-start.5 = (bf16[1024,512]{1,0:T(8,128)(2,1)S(1)}, bf16[1024,512]{1,0:T(8,128)(2,1)}, u32[]{:S(2)}, u32[]{:S(2)}) collective-permute-start(bf16[1024,512]{1,0:T(8,128)(2,1)S(1)} %copy-done), channel_id=1, source_target_pairs={{0,1},{1,0},{2,3},{3,2},{4,5},{5,4},{6,7},{7,6},{8,9},{9,8},{10,11... | collective-permute-start | bytes 3145736 | tf_op jit(solution)/shard_map/ppermute | solution.py:396
  13.7 21.4 %copy-start.6 = (s32[8,32,28]{1,0,2:T(8,128)S(1)}, s32[8,32,28]{1,0,2:T(8,128)}, u32[]{:S(2)}) copy-start(s32[8,32,28]{1,0,2:T(8,128)} %param.17) | copy-start | bytes 86020
  13.7 23.7 %copy-start.3 = (f32[64,64]{1,0:T(8,128)S(1)}, f32[64,64]{1,0:T(8,128)}, u32[]{:S(2)}) copy-start(f32[64,64]{1,0:T(8,128)} %constant.24.clone.refs_8_.refs_6_) | copy-start | bytes 49156
  13.7 23.7 %copy-start.5 = (s32[2]{0:T(128)S(1)}, s32[2]{0:T(128)}, u32[]{:S(2)}) copy-start(s32[2]{0:T(128)} %pad_add_fusion.2.ids_ref.refs_0_) | copy-start | bytes 28
  13.7 23.7 %collective-permute-start.3 = (bf16[1024,256]{1,0:T(8,128)(2,1)}, bf16[1024,256]{1,0:T(8,128)(2,1)}, u32[]{:S(2)}, u32[]{:S(2)}) collective-permute-start(bf16[1024,256]{1,0:T(8,128)(2,1)} %get-tuple-element.20), channel_id=1, source_target_pairs={{0,2},{1,3},{2,0},{3,1},{4,6},{5,7},{6,4},{7,5},{8,10},{9,11},{10,... | collective-permute-start | bytes 1572872 | tf_op jit(solution)/shard_map/ppermute | solution.py:396
  26.4 11.0 %collective-permute-start.7 = (bf16[1024,256]{1,0:T(8,128)(2,1)}, bf16[1024,256]{1,0:T(8,128)(2,1)}, u32[]{:S(2)}, u32[]{:S(2)}) collective-permute-start(bf16[1024,256]{1,0:T(8,128)(2,1)} %collective-permute-done.6.refs_4_), channel_id=1, source_target_pairs={{0,1},{1,0},{2,3},{3,2},{4,5},{5,4},{6,7},{7,6},{8,9},{9,8},{10,11... | collective-permute-start | bytes 1572872 | tf_op jit(solution)/shard_map/ppermute | solution.py:396
  34.5 63.3 %collective-permute-start = (f32[1024,512]{1,0:T(8,128)}, f32[1024,512]{1,0:T(8,128)S(1)}, u32[]{:S(2)}, u32[]{:S(2)}) collective-permute-start(f32[1024,512]{1,0:T(8,128)} %get-tuple-element.12), channel_id=1, source_target_pairs={{0,1},{1,0},{2,3},{3,2},{4,5},{5,4},{6,7},{7,6},{8,9},{9,8},{10,11... | collective-permute-start | bytes 6291464 | tf_op jit(solution)/shard_map/ppermute | solution.py:396
  37.4 31.4 %collective-permute-start.4 = (bf16[1024,256]{1,0:T(8,128)(2,1)}, bf16[1024,256]{1,0:T(8,128)(2,1)S(1)}, u32[]{:S(2)}, u32[]{:S(2)}) collective-permute-start(bf16[1024,256]{1,0:T(8,128)(2,1)} %collective-permute-done.3.refs_2_), channel_id=1, source_target_pairs={{0,1},{1,0},{2,3},{3,2},{4,5},{5,4},{6,7},{7,6},{8,9},{9,8},{10,11... | collective-permute-start | bytes 1572872 | tf_op jit(solution)/shard_map/ppermute | solution.py:396
  37.4 20.1 %copy-start.2 = (f32[1024,512]{1,0:T(8,128)S(1)}, f32[1024,512]{1,0:T(8,128)}, u32[]{:S(2)}) copy-start(f32[1024,512]{1,0:T(8,128)} %get-tuple-element.13.a_ref) | copy-start | bytes 6291460
  52.9 8.0 %collective-permute-start.14 = (s16[32,1792]{1,0:T(8,128)(2,1)S(1)}, s16[32,1792]{1,0:T(8,128)(2,1)S(1)}, u32[]{:S(2)}, u32[]{:S(2)}) collective-permute-start(s16[32,1792]{1,0:T(8,128)(2,1)S(1)} %get-tuple-element.18), channel_id=1, source_target_pairs={{0,24},{4,28},{8,16},{12,20},{16,8},{20,12},{24,0},{28,4},{1,25},{... | collective-permute-start | bytes 344072 | tf_op jit(solution)/shard_map/ppermute | solution.py:396
  56.8 10.3 %collective-permute-start.13 = (s16[32,1792]{1,0:T(8,128)(2,1)S(1)}, s16[32,1792]{1,0:T(8,128)(2,1)S(1)}, u32[]{:S(2)}, u32[]{:S(2)}) collective-permute-start(s16[32,1792]{1,0:T(8,128)(2,1)S(1)} %get-tuple-element.18), channel_id=1, source_target_pairs={{0,16},{4,20},{8,24},{12,28},{16,0},{20,4},{24,8},{28,12},{1,17},{... | collective-permute-start | bytes 344072 | tf_op jit(solution)/shard_map/ppermute | solution.py:396
  56.9 10.3 %collective-permute-start.12 = (s16[32,1792]{1,0:T(8,128)(2,1)S(1)}, s16[32,1792]{1,0:T(8,128)(2,1)S(1)}, u32[]{:S(2)}, u32[]{:S(2)}) collective-permute-start(s16[32,1792]{1,0:T(8,128)(2,1)S(1)} %get-tuple-element.18), channel_id=1, source_target_pairs={{0,8},{4,12},{8,0},{12,4},{16,24},{20,28},{24,16},{28,20},{1,9},{5... | collective-permute-start | bytes 344072 | tf_op jit(solution)/shard_map/ppermute | solution.py:396
  61.0 36.9 %collective-permute-start.2 = (s16[1056,512]{1,0:T(8,128)(2,1)}, s16[1056,512]{1,0:T(8,128)(2,1)}, u32[]{:S(2)}, u32[]{:S(2)}) collective-permute-start(s16[1056,512]{1,0:T(8,128)(2,1)} %add_encode.1), channel_id=1, source_target_pairs={{0,2},{1,3},{2,0},{3,1},{4,6},{5,7},{6,4},{7,5},{8,10},{9,11},{10,... | collective-permute-start | bytes 3244040 | tf_op jit(solution)/shard_map/ppermute | solution.py:396
  67.2 20.6 %collective-permute-start.15 = (s16[4,32,1792]{2,1,0:T(8,128)(2,1)S(1)}, s16[4,32,1792]{2,1,0:T(8,128)(2,1)S(1)}, u32[]{:S(2)}, u32[]{:S(2)}) collective-permute-start(s16[4,32,1792]{2,1,0:T(8,128)(2,1)S(1)} %pad_add_fusion.near_ref), channel_id=1, source_target_pairs={{0,4},{4,0},{8,12},{12,8},{16,20},{20,16},{24,28},{28,24},{1,5},{5... | collective-permute-start | bytes 1376264 | tf_op jit(solution)/shard_map/ppermute | solution.py:396
  68.8 19.0 %copy-start.4 = (bf16[64,192]{1,0:T(8,128)(2,1)S(1)}, bf16[64,192]{1,0:T(8,128)(2,1)}, u32[]{:S(2)}) copy-start(bf16[64,192]{1,0:T(8,128)(2,1)} %constant.31.ct_ref) | copy-start | bytes 73732
  77.0 6.0 %collective-permute-start.10 = (s16[16,1792]{1,0:T(8,128)(2,1)S(1)}, s16[16,1792]{1,0:T(8,128)(2,1)S(1)}, u32[]{:S(2)}, u32[]{:S(2)}) collective-permute-start(s16[16,1792]{1,0:T(8,128)(2,1)S(1)} %get-tuple-element.17), channel_id=1, source_target_pairs={{0,24},{4,28},{8,16},{12,20},{16,8},{20,12},{24,0},{28,4},{1,25},{... | collective-permute-start | bytes 172040 | tf_op jit(solution)/shard_map/ppermute | solution.py:396
  79.6 5.5 %collective-permute-start.9 = (s16[16,1792]{1,0:T(8,128)(2,1)S(1)}, s16[16,1792]{1,0:T(8,128)(2,1)S(1)}, u32[]{:S(2)}, u32[]{:S(2)}) collective-permute-start(s16[16,1792]{1,0:T(8,128)(2,1)S(1)} %get-tuple-element.17), channel_id=1, source_target_pairs={{0,16},{4,20},{8,24},{12,28},{16,0},{20,4},{24,8},{28,12},{1,17},{... | collective-permute-start | bytes 172040 | tf_op jit(solution)/shard_map/ppermute | solution.py:396
  83.0 4.2 %collective-permute-start.8 = (s16[16,1792]{1,0:T(8,128)(2,1)S(1)}, s16[16,1792]{1,0:T(8,128)(2,1)S(1)}, u32[]{:S(2)}, u32[]{:S(2)}) collective-permute-start(s16[16,1792]{1,0:T(8,128)(2,1)S(1)} %get-tuple-element.17), channel_id=1, source_target_pairs={{0,8},{4,12},{8,0},{12,4},{16,24},{20,28},{24,16},{28,20},{1,9},{5... | collective-permute-start | bytes 172040 | tf_op jit(solution)/shard_map/ppermute | solution.py:396
  87.2 7.3 %collective-permute-start.11 = (s16[4,16,1792]{2,1,0:T(8,128)(2,1)S(1)}, s16[4,16,1792]{2,1,0:T(8,128)(2,1)S(1)}, u32[]{:S(2)}, u32[]{:S(2)}) collective-permute-start(s16[4,16,1792]{2,1,0:T(8,128)(2,1)S(1)} %pad_add_fusion.1.near_ref), channel_id=1, source_target_pairs={{0,4},{4,0},{8,12},{12,8},{16,20},{20,16},{24,28},{28,24},{1,5},{5... | collective-permute-start | bytes 688136 | tf_op jit(solution)/shard_map/ppermute | solution.py:396
  94.5 3.3 %copy-start.1 = (f32[1024,512]{1,0:T(8,128)S(1)}, f32[1024,512]{1,0:T(8,128)}, u32[]{:S(2)}) copy-start(f32[1024,512]{1,0:T(8,128)} %get-tuple-element.11.a_ref) | copy-start | bytes 6291460
where the time goes:
time: 100 us
  Pallas kernels  55.1 us (55%)
  waiting for transfers between devices  25.4 us (25%)
  starting transfers between devices  15.1 us (15%)
  local copies, waits for them, and re-layouts  3 us (3%)
    ppermute x16, waiting for transfers between devices, flip(): return lax.ppermute(x, axis, [(i, i ^ mask) for i in range(size)])  25.4 us
    pallas_call x2, Pallas kernels, grad_call(): pl.pallas_call(functools.partial(grad_kernel, len(acts), places, per_owne...  23.7 us
    pallas_call x2, Pallas kernels, partial_call(): pl.pallas_call(functools.partial(partial_kernel, masks), grid_spec=pltpu....  16.4 us
    ppermute x16, starting transfers between devices, flip(): return lax.ppermute(x, axis, [(i, i ^ mask) for i in range(size)])  15.1 us
    pallas_call x2, Pallas kernels, update_call(): pl.pallas_call(functools.partial(update_kernel, places, per_owner, chaine...  9.93 us
    pallas_call x1, Pallas kernels, add_encode(): pl.pallas_call(add_encode_kernel, grid=(blocks,), in_specs=[spec, spec],...  2.83 us
    pallas_call x1, Pallas kernels, add_decode(): pl.pallas_call(add_decode_kernel, grid=(blocks,), in_specs=[spec, spec, p...  2.31 us
  transfers between devices with their start and end apart: 16, of which 6 were waited for; matrix products, arithmetic and copies ran while one was open for 3% of the time, Pallas kernels for 44%

commit v1 on v0

--- a/solution.py
+++ b/solution.py
@@ -11,6 +11,7 @@
 
 TILE = 64
 LANES = 128
+STRIP = 256
 STEP = 256
 PER_STEP = STEP // TILE
 PAD = 8
@@ -53,6 +54,30 @@
 
 def decode_block(whole, power):
     return whole * jnp.exp2(power)
+
+
+def encode_rows(values):
+    rows, hidden = values.shape
+    lane = lax.broadcasted_iota(jnp.int32, (rows, LANES), 1)
+    powers = jnp.zeros((rows, LANES), jnp.float32)
+    strips = []
+    for n in range(hidden // STRIP):
+        strip = values[:, n * STRIP : (n + 1) * STRIP]
+        largest = jnp.maximum(jnp.max(jnp.abs(strip), axis=1, keepdims=True), 1e-30)
+        power = jnp.ceil(jnp.log2(largest * (1.0 / 32767.0)))
+        strips.append(jnp.clip(jnp.round(strip * jnp.exp2(-power)), -32767.0, 32767.0))
+        powers = jnp.where(lane == n, power, powers)
+    return jnp.concatenate(strips + [powers], axis=1).astype(jnp.int32).astype(jnp.int16)
+
+
+def decode_rows(code):
+    code = code.astype(jnp.int32).astype(jnp.float32)
+    hidden = code.shape[1] - LANES
+    scale = jnp.exp2(code[:, hidden:])
+    strips = [
+        code[:, n * STRIP : (n + 1) * STRIP] * scale[:, n : n + 1] for n in range(hidden // STRIP)
+    ]
+    return jnp.concatenate(strips, axis=1)
 
 
 def block_of(ids_ref, place, per_owner):
@@ -66,7 +91,7 @@
     go_ref, mom_ref, ct_ref = refs[:3]
     refs = refs[4:] if chained else refs[3:]
     out_ref, code_ref = refs[:2]
-    go_buf, acts_buf, mom_buf, g_ref, tab_ref, rows_ref, in_sem, out_sem = refs[2:]
+    go_buf, acts_buf, mom_buf, *g_refs, turned_ref, tab_ref, rows_ref, in_sem, out_sem = refs[2:]
     steps = len(places)
     _, hidden = go_buf.shape
 
@@ -88,37 +113,48 @@
         tab_ref[k] = jnp.broadcast_to(ct_ref[:, k : k + 1], (TILE, LANES))
     left = lax.broadcasted_iota(jnp.int32, (TILE, LANES), 1) < TILE
     go_copy.wait()
+
+    def wait_for(buf, sem):
+        pltpu.make_async_copy(buf, buf, sem).wait()
+
+    def turn(step):
+        wait_for(acts_buf.at[step], in_sem.at[step])
+        turned_ref[...] = jnp.transpose(acts_buf[step])
+
+    def products(step, lanes):
+        g_refs[step % 2][:, lanes] = jnp.dot(
+            turned_ref[...], go_buf[:, lanes], preferred_element_type=jnp.float32
+        )
+
+    strips = [pl.ds(n * STRIP, STRIP) for n in range(hidden // STRIP)]
+    turn(0)
+    for strip in strips:
+        products(0, strip)
     for step in range(steps):
-        here = acts_buf.at[step]
-        pltpu.make_async_copy(here, here, in_sem.at[step]).wait()
-        g_ref[...] = lax.dot_general(
-            acts_buf[step], go_buf[...], (((0,), (0,)), ((), ())), preferred_element_type=jnp.float32
-        )
-        here = mom_buf.at[step]
-        pltpu.make_async_copy(here, here, in_sem.at[steps + step]).wait()
+        wait_for(mom_buf.at[step], in_sem.at[steps + step])
+        if step + 1 < steps:
+            turn(step + 1)
         block = block_of(ids_ref, places[step], per_owner)
-
-        def tile_row(tr, carry):
-            rows = pl.ds(pl.multiple_of(tr * TILE, TILE), TILE)
-            tile = block * PER_STEP + tr
-            for pair in range(hidden // LANES):
-                lanes = pl.ds(pair * LANES, LANES)
-                picked = jnp.where(
-                    left,
-                    tab_ref[chosen_ref[tile, 2 * pair]],
-                    tab_ref[chosen_ref[tile, 2 * pair + 1]],
-                )
-                kept = decay_rate * mom_buf[step, rows, lanes] + g_ref[rows, lanes]
-                row = jnp.sum(kept * picked, axis=0, keepdims=True)
-                mom_buf[step, rows, lanes] = kept - picked * row
-                rows_ref[step * PER_STEP + tr, :, lanes] = row
-            return carry
-
-        lax.fori_loop(0, PER_STEP, tile_row, 0)
+        g_ref = g_refs[step % 2]
+        for n, strip in enumerate(strips):
+            if step + 1 < steps:
+                products(step + 1, strip)
+            for tr in range(PER_STEP):
+                rows = pl.ds(tr * TILE, TILE)
+                tile = block * PER_STEP + tr
+                for pair in range(n * STRIP // LANES, (n + 1) * STRIP // LANES):
+                    lanes = pl.ds(pair * LANES, LANES)
+                    picked = jnp.where(
+                        left,
+                        tab_ref[chosen_ref[tile, 2 * pair]],
+                        tab_ref[chosen_ref[tile, 2 * pair + 1]],
+                    )
+                    kept = decay_rate * mom_buf[step, rows, lanes] + g_ref[rows, lanes]
+                    row = jnp.sum(kept * picked, axis=0, keepdims=True)
+                    mom_buf[step, rows, lanes] = kept - picked * row
+                    rows_ref[step * PER_STEP + tr, :, lanes] = row
         pltpu.make_async_copy(mom_buf.at[step], out_ref.at[rows_of(step), :], out_sem.at[step]).start()
-    whole, power = encode(jnp.concatenate([rows_ref[n] for n in range(steps * PER_STEP)], axis=0))
-    power = jnp.broadcast_to(power, (PAD, power.shape[1]))
-    code_ref[...] = jnp.concatenate([whole, power], axis=0).astype(jnp.int32).astype(jnp.int16)
+    code_ref[...] = encode_rows(jnp.concatenate([rows_ref[n] for n in range(steps * PER_STEP)], axis=0))
     for step in range(steps):
         pltpu.make_async_copy(mom_buf.at[step], out_ref.at[rows_of(step), :], out_sem.at[step]).wait()
 
@@ -144,12 +180,14 @@
             num_scalar_prefetch=2,
             grid=(1,),
             in_specs=in_specs,
-            out_specs=[far, pl.BlockSpec((rows + PAD, hidden), lambda i, ids, cho: (0, 0))],
+            out_specs=[far, pl.BlockSpec((rows, hidden + LANES), lambda i, ids, cho: (0, 0))],
             scratch_shapes=[
                 pltpu.VMEM((tokens, hidden), grad_out.dtype),
                 pltpu.VMEM((steps, tokens, STEP), grad_out.dtype),
                 pltpu.VMEM((steps, STEP, hidden), jnp.float32),
                 pltpu.VMEM((STEP, hidden), jnp.float32),
+                pltpu.VMEM((STEP, hidden), jnp.float32),
+                pltpu.VMEM((STEP, tokens), grad_out.dtype),
                 pltpu.VMEM((TILE, TILE, LANES), jnp.float32),
                 pltpu.VMEM((rows + PAD, 1, hidden), jnp.float32),
                 pltpu.SemaphoreType.DMA((2 * steps + 1,)),
@@ -158,7 +196,7 @@
         ),
         out_shape=[
             jax.ShapeDtypeStruct((features, hidden), jnp.float32),
-            jax.ShapeDtypeStruct((rows + PAD, hidden), jnp.int16),
+            jax.ShapeDtypeStruct((rows, hidden + LANES), jnp.int16),
         ],
         input_output_aliases=aliases,
         cost_estimate=pl.CostEstimate(
@@ -294,8 +332,7 @@
     replicas = 2 * total
     for side, ref in enumerate((near_ref, far_ref)):
         for slot in range(total):
-            code = ref[slot].astype(jnp.int32).astype(jnp.float32)
-            values = decode_block(code[:rows], code[rows : rows + 1])
+            values = decode_rows(ref[slot])
             start = pl.multiple_of((ids_ref[1] ^ (2 * slot + side)) * rows, 8)
             for strip in range(hidden // LANES):
                 held_ref[strip, pl.ds(start, rows), :] = values[:, strip * LANES : (strip + 1) * LANES]
@@ -348,7 +385,7 @@
 
 
 def update_call(places, ids, near, far, freq_lanes, features, per_owner, chained):
-    hidden = near.shape[2]
+    hidden = near.shape[2] - LANES
     steps = len(places)
     rows = steps * PER_STEP
     anywhere = pl.BlockSpec(memory_space=pltpu.HBM)
@@ -410,42 +447,40 @@
     tile_rows, tile_cols = freq_rows.shape[1:]
     replicas = freq_rows.shape[0]
 
-    chunks = [activations[:, n * STEP : (n + 1) * STEP] for n in range(per_owner)]
     twin = flip(activations, "tensor", 1)
-    across = [flip(chunk, "tensor", 2) for chunk in chunks]
-    across_twin = [flip(chunk, "tensor", 1) for chunk in across]
+    across = flip(activations, "tensor", 2)
+    across_twin = flip(across, "tensor", 1)
+    sources = ((activations, twin), (across, across_twin))
 
     for_twin, for_far = partial_call((3, 2), ids, grad_out, weight, width)
     received = flip(for_twin, "tensor", 1)
-    code = add_encode(for_far, received, 2)
-    code = flip(code, "tensor", 2)
-    for_twin, own = partial_call((1, 0), ids, grad_out, weight, width)
-    own_twin = flip(for_twin, "tensor", 1)
-
-    chosen = lax.dynamic_index_in_dim(freq_rows, replica, 0, keepdims=False)
-    kept = momentum[0]
-    places = [
-        tuple((mask, n) for mask in (0, 1) for n in range(per_owner)) + ((2, 0), (3, 0)),
-    ] + [((2, n), (3, n)) for n in range(1, per_owner)]
-    out = None
-    codes = []
-    for n in range(per_owner):
-        acts = [across[n], across_twin[n]]
-        if n == 0:
-            acts = [activations, twin] + acts
-        out, coded = grad_call(places[n], ids, chosen, acts, grad_out, kept, per_owner, out)
-        codes.append(coded)
-
     lanes = freq_rows.reshape(replicas, tile_rows, tile_cols // 4, 1, 4)
     lanes = jnp.transpose(lanes, (1, 2, 3, 4, 0))
     lanes = jnp.broadcast_to(lanes, (tile_rows, tile_cols // 4, 4, 4, replicas))
     lanes = lanes.reshape(tile_rows, tile_cols // 4 * 16 * replicas)
     lanes = jnp.pad(lanes, ((0, PAD), (0, 0)))
+    chosen = lax.dynamic_index_in_dim(freq_rows, replica, 0, keepdims=False)
+    received, lanes = lax.optimization_barrier((received, lanes))
+    code = add_encode(for_far, received, 2)
+    code = flip(code, "tensor", 2)
+    for_twin, own = partial_call((1, 0), ids, grad_out, weight, width)
+    own_twin = flip(for_twin, "tensor", 1)
+
+    kept = momentum[0]
+    places = [
+        tuple((mask, n) for mask in masks for n in range(per_owner)) for masks in ((0, 1), (2, 3))
+    ]
+    out = None
+    codes = []
+    for half, acts in enumerate(sources):
+        out, coded = grad_call(places[half], ids, chosen, acts, grad_out, kept, per_owner, out)
+        codes.append(coded)
+
     update = None
-    for n in range(per_owner):
-        near = jnp.stack([codes[n]] + [flip(codes[n], "replica", mask) for mask in range(2, replicas, 2)])
+    for half in range(2):
+        near = jnp.stack([codes[half]] + [flip(codes[half], "replica", mask) for mask in range(2, replicas, 2)])
         far = flip(near, "replica", 1)
-        update = update_call(places[n], ids, near, far, lanes, features, per_owner, update)
+        update = update_call(places[half], ids, near, far, lanes, features, per_owner, update)
 
     input_grad = add_decode(own, own_twin, code, 2)
     return (input_grad, out[None], update)
@@ -504,7 +539,8 @@
         and sizes["replica"] == 8
         and tokens % 32 == 0
         and width == 2 * STEP
-        and hidden % (4 * TILE) == 0
+        and hidden % STRIP == 0
+        and hidden <= STRIP * LANES
     )
 
 

time: 100 us -> 96.6 us (0.966)
  waiting for transfers between devices: 25.4 us -> 21.2 us
  starting transfers between devices: 15.1 us -> 18 us
  Pallas kernels: 55.1 us -> 53.6 us
    ppermute x16 -> x14, waiting for transfers between devices: 25.4 us -> 21.2 us  [flip(): return lax.ppermute(x, axis, [(i, i ^ mask) for i in range(size)])]
    ppermute x16 -> x14, starting transfers between devices: 15.1 us -> 18 us  [flip(): return lax.ppermute(x, axis, [(i, i ^ mask) for i in range(size)])]
    pallas_call x1, Pallas kernels: 2.31 us -> 1.29 us  [add_decode(): pl.pallas_call(add_decode_kernel, grid=(blocks,), in_specs=[spec, spec, p...]
  transfers between devices with their start and end apart: 16 -> 14, of which waited for: 6 -> 4; matrix products, arithmetic and copies ran while one was open for 3% -> 3% of each run, Pallas kernels for 44% -> 54%
where the time goes in v1:
time: 96.6 us; the launch traced here: 96.4 us
  Pallas kernels  53.6 us (55%)
  waiting for transfers between devices  21.2 us (22%)
  starting transfers between devices  18 us (19%)
  local copies, waits for them, and re-layouts  2.15 us (2%)
    pallas_call x2, Pallas kernels, grad_call(): pl.pallas_call(functools.partial(grad_kernel, len(acts), places, per_owne...  23.7 us
    ppermute x14, waiting for transfers between devices, flip(): return lax.ppermute(x, axis, [(i, i ^ mask) for i in range(size)])  21.2 us
    ppermute x14, starting transfers between devices, flip(): return lax.ppermute(x, axis, [(i, i ^ mask) for i in range(size)])  18 us
    pallas_call x2, Pallas kernels, partial_call(): pl.pallas_call(functools.partial(partial_kernel, masks), grid_spec=pltpu....  16.4 us
    pallas_call x2, Pallas kernels, update_call(): pl.pallas_call(functools.partial(update_kernel, places, per_owner, chaine...  10.1 us
    pallas_call x1, Pallas kernels, add_encode(): pl.pallas_call(add_encode_kernel, grid=(blocks,), in_specs=[spec, spec],...  2.07 us
  transfers between devices with their start and end apart: 14, of which 4 were waited for; matrix products, arithmetic and copies ran while one was open for 3% of the time, Pallas kernels for 54%

profile of v1, /device:TPU:0, one launch (start us, length us, event | category | flops | bytes accessed | tf_op | source)
XLA Modules:
  0.0 96.4 jit_solution(13480043506385301656)
XLA Ops:
  0.6 3.0 %collective-permute-start.3 = (bf16[1024,512]{1,0:T(8,128)(2,1)}, bf16[1024,512]{1,0:T(8,128)(2,1)}, u32[]{:S(2)}, u32[]{:S(2)}) collective-permute-start(bf16[1024,512]{1,0:T(8,128)(2,1)} %refs_2_.1), channel_id=1, source_target_pairs={{0,2},{1,3},{2,0},{3,1},{4,6},{5,7},{6,4},{7,5},{8,10},{9,11},{10,... | collective-permute-start | bytes 3145736 | tf_op jit(solution)/shard_map/ppermute | solution.py:433
  3.7 0.6 pad_add_fusion.2.ids_ref.refs_0_
  4.2 8.3 %partial_products.3 = (f32[1024,512]{1,0:T(8,128)}, f32[1024,512]{1,0:T(8,128)}) custom-call(s32[2]{0:T(128)} %pad_add_fusion.2.ids_ref.refs_0_, bf16[1024,1792]{1,0:T(8,128)(2,1)} %refs_4_.3, bf16[2048,1792]{1,0:T(8,128)(2,1)} %w_ref.3), custom_call_target="tpu_custom_call" | custom-call | flops 3758096384 | bytes 11534336 | tf_op jit(solution)/shard_map/partial_products/pallas_call | solution.py:249
  12.5 0.0 copy-start.6
  12.6 0.0 copy-start.4
  12.6 0.0 copy-start.5
  12.6 0.1 collective-permute-start.1
  12.7 0.0 copy-done.2
  12.7 0.5 collective-permute-start.5
  13.2 14.0 %collective-permute-done.3.refs_2_ = bf16[1024,512]{1,0:T(8,128)(2,1)} collective-permute-done((bf16[1024,512]{1,0:T(8,128)(2,1)}, bf16[1024,512]{1,0:T(8,128)(2,1)}, u32[]{:S(2)}, u32[]{:S(2)}) %collective-permute-start.3) | collective-permute-done | bytes 1048608 | tf_op jit(solution)/shard_map/ppermute | solution.py:433
  27.1 0.0 collective-permute-start.4
  27.1 8.1 %partial_products.2 = (f32[1024,512]{1,0:T(8,128)}, f32[1024,512]{1,0:T(8,128)}) custom-call(s32[2]{0:T(128)} %pad_add_fusion.2.ids_ref.refs_0_, bf16[1024,1792]{1,0:T(8,128)(2,1)} %refs_4_.3, bf16[2048,1792]{1,0:T(8,128)(2,1)} %w_ref.3), custom_call_target="tpu_custom_call" | custom-call | flops 3758096384 | bytes 11534336 | tf_op jit(solution)/shard_map/partial_products/pallas_call | solution.py:249
  35.3 0.6 collective-permute-start
  35.9 0.1 copy.21
  36.0 0.8 broadcast_in_dim.11
  36.8 1.2 %copy.20 = s32[32,896]{1,0:T(8,128)S(1)} copy(s32[32,896]{0,1:T(8,128)} %bitcast.26) | data formatting | bytes 229376 | tf_op jit(solution)/shard_map/reshape | solution.py:460
  38.0 0.0 collective-permute-done.5.refs_3_
  38.0 0.0 copy-done.4
  38.0 0.0 copy-done.5
  38.0 0.0 copy-start.1
  38.0 11.8 %grad_step.2 = (f32[2048,1792]{1,0:T(8,128)}, s16[16,1920]{1,0:T(8,128)(2,1)S(1)}) custom-call(s32[2]{0:T(128)S(1)} %copy-done.5, s32[32,28]{1,0:T(8,128)S(1)} %bitcast.19, bf16[1024,512]{1,0:T(8,128)(2,1)S(1)} %copy-done.2, bf16[1024,512]{1,0:T(8,128)(2,1)} %collective-permute-done.5.refs_3_, bf16[1024,1792]{1,0:T(8,128)(2,1)} %refs_4_.3, ...), custom_call_target="tpu_custom_call" | custom-call | flops 3758096384 | bytes 18350080 | tf_op jit(solution)/shard_map/grad_step/pallas_call | solution.py:177
  49.8 3.9 %collective-permute-start.12 = (s16[16,1920]{1,0:T(8,128)(2,1)S(1)}, s16[16,1920]{1,0:T(8,128)(2,1)S(1)}, u32[]{:S(2)}, u32[]{:S(2)}) collective-permute-start(s16[16,1920]{1,0:T(8,128)(2,1)S(1)} %get-tuple-element.22), channel_id=1, source_target_pairs={{0,24},{4,28},{8,16},{12,20},{16,8},{20,12},{24,0},{28,4},{1,25},{... | collective-permute-start | bytes 184328 | tf_op jit(solution)/shard_map/ppermute | solution.py:433
  53.8 0.0 collective-permute-start.11
  53.8 0.0 collective-permute-done.1.b_ref
  53.8 0.6 collective-permute-start.10
  54.4 0.0 copy-done.1
  54.4 2.1 %add_encode.1 = s16[1056,512]{1,0:T(8,128)(2,1)S(1)} custom-call(f32[1024,512]{1,0:T(8,128)S(1)} %copy-done.1, f32[1024,512]{1,0:T(8,128)} %collective-permute-done.1.b_ref), custom_call_target="tpu_custom_call" | custom-call | flops 4194304 | bytes 5242880 | tf_op jit(solution)/shard_map/add_encode/pallas_call | solution.py:289
  56.5 0.0 collective-permute-done.4.refs_3_
  56.5 1.7 %collective-permute-start.2 = (s16[1056,512]{1,0:T(8,128)(2,1)S(1)}, s16[1056,512]{1,0:T(8,128)(2,1)S(1)}, u32[]{:S(2)}, u32[]{:S(2)}) collective-permute-start(s16[1056,512]{1,0:T(8,128)(2,1)S(1)} %add_encode.1), channel_id=1, source_target_pairs={{0,2},{1,3},{2,0},{3,1},{4,6},{5,7},{6,4},{7,5},{8,10},{9,11},{10,... | collective-permute-start | bytes 3244040 | tf_op jit(solution)/shard_map/ppermute | solution.py:433
  58.2 11.9 %grad_step.3 = (f32[2048,1792]{1,0:T(8,128)}, s16[16,1920]{1,0:T(8,128)(2,1)S(1)}) custom-call(s32[2]{0:T(128)S(1)} %copy-done.5, s32[32,28]{1,0:T(8,128)S(1)} %bitcast.20, bf16[1024,512]{1,0:T(8,128)(2,1)} %collective-permute-done.3.refs_2_, bf16[1024,512]{1,0:T(8,128)(2,1)} %collective-permute-done.4.refs_3_, ...), custom_call_target="tpu_custom_call", output_to_operand_aliasing={{0}: (7, {})} | custom-call | flops 3758096384 | bytes 18350080 | tf_op jit(solution)/shard_map/grad_step/pallas_call | solution.py:177
  70.1 0.0 collective-permute-done.12
  70.2 3.6 %collective-permute-start.8 = (s16[16,1920]{1,0:T(8,128)(2,1)S(1)}, s16[16,1920]{1,0:T(8,128)(2,1)S(1)}, u32[]{:S(2)}, u32[]{:S(2)}) collective-permute-start(s16[16,1920]{1,0:T(8,128)(2,1)S(1)} %get-tuple-element.20), channel_id=1, source_target_pairs={{0,24},{4,28},{8,16},{12,20},{16,8},{20,12},{24,0},{28,4},{1,25},{... | collective-permute-start | bytes 184328 | tf_op jit(solution)/shard_map/ppermute | solution.py:433
  73.8 0.0 collective-permute-done.11
  73.8 0.0 collective-permute-start.7
  73.8 0.0 collective-permute-done.10
  73.8 0.8 collective-permute-start.6
  74.6 1.7 %collective-permute-done.8 = s16[16,1920]{1,0:T(8,128)(2,1)S(1)} collective-permute-done((s16[16,1920]{1,0:T(8,128)(2,1)S(1)}, s16[16,1920]{1,0:T(8,128)(2,1)S(1)}, u32[]{:S(2)}, u32[]{:S(2)}) %collective-permute-start.8) | collective-permute-done | bytes 61472 | tf_op jit(solution)/shard_map/ppermute | solution.py:433
  76.3 1.5 %collective-permute-start.13 = (s16[4,16,1920]{2,1,0:T(8,128)(2,1)S(1)}, s16[4,16,1920]{2,1,0:T(8,128)(2,1)S(1)}, u32[]{:S(2)}, u32[]{:S(2)}) collective-permute-start(s16[4,16,1920]{2,1,0:T(8,128)(2,1)S(1)} %pad_add_fusion.1.near_ref), channel_id=1, source_target_pairs={{0,4},{4,0},{8,12},{12,8},{16,20},{20,16},{24,28},{28,24},{1,5},{5... | collective-permute-start | bytes 737288 | tf_op jit(solution)/shard_map/ppermute | solution.py:433
  77.9 1.1 %collective-permute-done.7 = s16[16,1920]{1,0:T(8,128)(2,1)S(1)} collective-permute-done((s16[16,1920]{1,0:T(8,128)(2,1)S(1)}, s16[16,1920]{1,0:T(8,128)(2,1)S(1)}, u32[]{:S(2)}, u32[]{:S(2)}) %collective-permute-start.7) | collective-permute-done | bytes 61472 | tf_op jit(solution)/shard_map/ppermute | solution.py:433
  78.9 0.0 collective-permute-done.6
  79.0 1.6 %collective-permute-start.9 = (s16[4,16,1920]{2,1,0:T(8,128)(2,1)S(1)}, s16[4,16,1920]{2,1,0:T(8,128)(2,1)S(1)}, u32[]{:S(2)}, u32[]{:S(2)}) collective-permute-start(s16[4,16,1920]{2,1,0:T(8,128)(2,1)S(1)} %pad_add_fusion.near_ref), channel_id=1, source_target_pairs={{0,4},{4,0},{8,12},{12,8},{16,20},{20,16},{24,28},{28,24},{1,5},{5... | collective-permute-start | bytes 737288 | tf_op jit(solution)/shard_map/ppermute | solution.py:433
  80.6 4.4 %collective-permute-done.13.far_ref = s16[4,16,1920]{2,1,0:T(8,128)(2,1)S(1)} collective-permute-done((s16[4,16,1920]{2,1,0:T(8,128)(2,1)S(1)}, s16[4,16,1920]{2,1,0:T(8,128)(2,1)S(1)}, u32[]{:S(2)}, u32[]{:S(2)}) %collective-permute-start.13) | collective-permute-done | bytes 245792 | tf_op jit(solution)/shard_map/ppermute | solution.py:433
  84.9 5.0 %update_rows.2.refs_0_ = bf16[2048,1792]{1,0:T(8,128)(2,1)} custom-call(s32[2]{0:T(128)S(1)} %copy-done.5, s16[4,16,1920]{2,1,0:T(8,128)(2,1)S(1)} %pad_add_fusion.1.near_ref, s16[4,16,1920]{2,1,0:T(8,128)(2,1)S(1)} %collective-permute-done.13.far_ref, s32[40,896]{1,0:T(8,128)S(1)} %pad.4.freq_ref, bf16[64,192]{1,0:T(8,128)(2,1)S(1)} %copy-done.3), custom_call_target="tpu_custom_call" | custom-call | flops 1879048192 | bytes 3670016 | tf_op jit(solution)/shard_map/update_rows/pallas_call | solution.py:406
  90.0 0.0 collective-permute-done.9.far_ref
  90.0 5.0 %update_rows.3 = bf16[2048,1792]{1,0:T(8,128)(2,1)} custom-call(s32[2]{0:T(128)S(1)} %copy-done.5, s16[4,16,1920]{2,1,0:T(8,128)(2,1)S(1)} %pad_add_fusion.near_ref, s16[4,16,1920]{2,1,0:T(8,128)(2,1)S(1)} %collective-permute-done.9.far_ref, s32[40,896]{1,0:T(8,128)S(1)} %pad.4.freq_ref, ...), custom_call_target="tpu_custom_call", output_to_operand_aliasing={{}: (5, {})} | custom-call | flops 1879048192 | bytes 3670016 | tf_op jit(solution)/shard_map/update_rows/pallas_call | solution.py:406
  95.0 0.0 collective-permute-done.b_ref
  95.1 0.0 collective-permute-done.2.code_ref
  95.1 1.3 %add_decode.1 = bf16[1024,512]{1,0:T(8,128)(2,1)} custom-call(f32[1024,512]{1,0:T(8,128)S(1)} %copy-done, f32[1024,512]{1,0:T(8,128)S(1)} %collective-permute-done.b_ref, s16[1056,512]{1,0:T(8,128)(2,1)S(1)} %collective-permute-done.2.code_ref), custom_call_target="tpu_custom_call" | custom-call | flops 4194304 | bytes 6291456 | tf_op jit(solution)/shard_map/add_decode/pallas_call | solution.py:312
  (10 shorter events, 0.1 us)
Async XLA Ops:
  0.6 26.5 %collective-permute-start.3 = (bf16[1024,512]{1,0:T(8,128)(2,1)}, bf16[1024,512]{1,0:T(8,128)(2,1)}, u32[]{:S(2)}, u32[]{:S(2)}) collective-permute-start(bf16[1024,512]{1,0:T(8,128)(2,1)} %refs_2_.1), channel_id=1, source_target_pairs={{0,2},{1,3},{2,0},{3,1},{4,6},{5,7},{6,4},{7,5},{8,10},{9,11},{10,... | collective-permute-start | bytes 3145736 | tf_op jit(solution)/shard_map/ppermute | solution.py:433
  4.2 8.4 %copy-start.2 = (bf16[1024,512]{1,0:T(8,128)(2,1)S(1)}, bf16[1024,512]{1,0:T(8,128)(2,1)}, u32[]{:S(2)}) copy-start(bf16[1024,512]{1,0:T(8,128)(2,1)} %refs_2_.1) | copy-start | bytes 3145732
  12.5 23.3 %copy-start.6 = (s32[8,32,28]{1,0,2:T(8,128)S(1)}, s32[8,32,28]{1,0,2:T(8,128)}, u32[]{:S(2)}) copy-start(s32[8,32,28]{1,0,2:T(8,128)} %param.17) | copy-start | bytes 86020
  12.6 25.5 %copy-start.4 = (f32[64,64]{1,0:T(8,128)S(1)}, f32[64,64]{1,0:T(8,128)}, u32[]{:S(2)}) copy-start(f32[64,64]{1,0:T(8,128)} %constant.24.clone.refs_6_) | copy-start | bytes 49156
  12.6 25.4 %copy-start.5 = (s32[2]{0:T(128)S(1)}, s32[2]{0:T(128)}, u32[]{:S(2)}) copy-start(s32[2]{0:T(128)} %pad_add_fusion.2.ids_ref.refs_0_) | copy-start | bytes 28
  12.6 41.2 %collective-permute-start.1 = (f32[1024,512]{1,0:T(8,128)}, f32[1024,512]{1,0:T(8,128)}, u32[]{:S(2)}, u32[]{:S(2)}) collective-permute-start(f32[1024,512]{1,0:T(8,128)} %get-tuple-element.16), channel_id=1, source_target_pairs={{0,1},{1,0},{2,3},{3,2},{4,5},{5,4},{6,7},{7,6},{8,9},{9,8},{10,11... | collective-permute-start | bytes 6291464 | tf_op jit(solution)/shard_map/ppermute | solution.py:433
  12.7 25.3 %collective-permute-start.5 = (bf16[1024,512]{1,0:T(8,128)(2,1)S(1)}, bf16[1024,512]{1,0:T(8,128)(2,1)}, u32[]{:S(2)}, u32[]{:S(2)}) collective-permute-start(bf16[1024,512]{1,0:T(8,128)(2,1)S(1)} %copy-done.2), channel_id=1, source_target_pairs={{0,1},{1,0},{2,3},{3,2},{4,5},{5,4},{6,7},{7,6},{8,9},{9,8},{10,11... | collective-permute-start | bytes 3145736 | tf_op jit(solution)/shard_map/ppermute | solution.py:433
  27.1 29.4 %collective-permute-start.4 = (bf16[1024,512]{1,0:T(8,128)(2,1)}, bf16[1024,512]{1,0:T(8,128)(2,1)}, u32[]{:S(2)}, u32[]{:S(2)}) collective-permute-start(bf16[1024,512]{1,0:T(8,128)(2,1)} %collective-permute-done.3.refs_2_), channel_id=1, source_target_pairs={{0,1},{1,0},{2,3},{3,2},{4,5},{5,4},{6,7},{7,6},{8,9},{9,8},{10,11... | collective-permute-start | bytes 3145736 | tf_op jit(solution)/shard_map/ppermute | solution.py:433
  35.3 59.8 %collective-permute-start = (f32[1024,512]{1,0:T(8,128)}, f32[1024,512]{1,0:T(8,128)S(1)}, u32[]{:S(2)}, u32[]{:S(2)}) collective-permute-start(f32[1024,512]{1,0:T(8,128)} %get-tuple-element.14), channel_id=1, source_target_pairs={{0,1},{1,0},{2,3},{3,2},{4,5},{5,4},{6,7},{7,6},{8,9},{9,8},{10,11... | collective-permute-start | bytes 6291464 | tf_op jit(solution)/shard_map/ppermute | solution.py:433
  38.0 16.4 %copy-start.1 = (f32[1024,512]{1,0:T(8,128)S(1)}, f32[1024,512]{1,0:T(8,128)}, u32[]{:S(2)}) copy-start(f32[1024,512]{1,0:T(8,128)} %get-tuple-element.15.a_ref) | copy-start | bytes 6291460
  49.8 20.3 %collective-permute-start.12 = (s16[16,1920]{1,0:T(8,128)(2,1)S(1)}, s16[16,1920]{1,0:T(8,128)(2,1)S(1)}, u32[]{:S(2)}, u32[]{:S(2)}) collective-permute-start(s16[16,1920]{1,0:T(8,128)(2,1)S(1)} %get-tuple-element.22), channel_id=1, source_target_pairs={{0,24},{4,28},{8,16},{12,20},{16,8},{20,12},{24,0},{28,4},{1,25},{... | collective-permute-start | bytes 184328 | tf_op jit(solution)/shard_map/ppermute | solution.py:433
  53.8 20.0 %collective-permute-start.11 = (s16[16,1920]{1,0:T(8,128)(2,1)S(1)}, s16[16,1920]{1,0:T(8,128)(2,1)S(1)}, u32[]{:S(2)}, u32[]{:S(2)}) collective-permute-start(s16[16,1920]{1,0:T(8,128)(2,1)S(1)} %get-tuple-element.22), channel_id=1, source_target_pairs={{0,16},{4,20},{8,24},{12,28},{16,0},{20,4},{24,8},{28,12},{1,17},{... | collective-permute-start | bytes 184328 | tf_op jit(solution)/shard_map/ppermute | solution.py:433
  53.8 20.0 %collective-permute-start.10 = (s16[16,1920]{1,0:T(8,128)(2,1)S(1)}, s16[16,1920]{1,0:T(8,128)(2,1)S(1)}, u32[]{:S(2)}, u32[]{:S(2)}) collective-permute-start(s16[16,1920]{1,0:T(8,128)(2,1)S(1)} %get-tuple-element.22), channel_id=1, source_target_pairs={{0,8},{4,12},{8,0},{12,4},{16,24},{20,28},{24,16},{28,20},{1,9},{5... | collective-permute-start | bytes 184328 | tf_op jit(solution)/shard_map/ppermute | solution.py:433
  56.5 38.6 %collective-permute-start.2 = (s16[1056,512]{1,0:T(8,128)(2,1)S(1)}, s16[1056,512]{1,0:T(8,128)(2,1)S(1)}, u32[]{:S(2)}, u32[]{:S(2)}) collective-permute-start(s16[1056,512]{1,0:T(8,128)(2,1)S(1)} %add_encode.1), channel_id=1, source_target_pairs={{0,2},{1,3},{2,0},{3,1},{4,6},{5,7},{6,4},{7,5},{8,10},{9,11},{10,... | collective-permute-start | bytes 3244040 | tf_op jit(solution)/shard_map/ppermute | solution.py:433
  58.2 26.7 %copy-start.3 = (bf16[64,192]{1,0:T(8,128)(2,1)S(1)}, bf16[64,192]{1,0:T(8,128)(2,1)}, u32[]{:S(2)}) copy-start(bf16[64,192]{1,0:T(8,128)(2,1)} %constant.31.ct_ref) | copy-start | bytes 73732
  70.2 6.2 %collective-permute-start.8 = (s16[16,1920]{1,0:T(8,128)(2,1)S(1)}, s16[16,1920]{1,0:T(8,128)(2,1)S(1)}, u32[]{:S(2)}, u32[]{:S(2)}) collective-permute-start(s16[16,1920]{1,0:T(8,128)(2,1)S(1)} %get-tuple-element.20), channel_id=1, source_target_pairs={{0,24},{4,28},{8,16},{12,20},{16,8},{20,12},{24,0},{28,4},{1,25},{... | collective-permute-start | bytes 184328 | tf_op jit(solution)/shard_map/ppermute | solution.py:433
  73.8 5.1 %collective-permute-start.7 = (s16[16,1920]{1,0:T(8,128)(2,1)S(1)}, s16[16,1920]{1,0:T(8,128)(2,1)S(1)}, u32[]{:S(2)}, u32[]{:S(2)}) collective-permute-start(s16[16,1920]{1,0:T(8,128)(2,1)S(1)} %get-tuple-element.20), channel_id=1, source_target_pairs={{0,16},{4,20},{8,24},{12,28},{16,0},{20,4},{24,8},{28,12},{1,17},{... | collective-permute-start | bytes 184328 | tf_op jit(solution)/shard_map/ppermute | solution.py:433
  73.8 5.1 %collective-permute-start.6 = (s16[16,1920]{1,0:T(8,128)(2,1)S(1)}, s16[16,1920]{1,0:T(8,128)(2,1)S(1)}, u32[]{:S(2)}, u32[]{:S(2)}) collective-permute-start(s16[16,1920]{1,0:T(8,128)(2,1)S(1)} %get-tuple-element.20), channel_id=1, source_target_pairs={{0,8},{4,12},{8,0},{12,4},{16,24},{20,28},{24,16},{28,20},{1,9},{5... | collective-permute-start | bytes 184328 | tf_op jit(solution)/shard_map/ppermute | solution.py:433
  76.3 8.6 %collective-permute-start.13 = (s16[4,16,1920]{2,1,0:T(8,128)(2,1)S(1)}, s16[4,16,1920]{2,1,0:T(8,128)(2,1)S(1)}, u32[]{:S(2)}, u32[]{:S(2)}) collective-permute-start(s16[4,16,1920]{2,1,0:T(8,128)(2,1)S(1)} %pad_add_fusion.1.near_ref), channel_id=1, source_target_pairs={{0,4},{4,0},{8,12},{12,8},{16,20},{20,16},{24,28},{28,24},{1,5},{5... | collective-permute-start | bytes 737288 | tf_op jit(solution)/shard_map/ppermute | solution.py:433
  79.0 11.0 %collective-permute-start.9 = (s16[4,16,1920]{2,1,0:T(8,128)(2,1)S(1)}, s16[4,16,1920]{2,1,0:T(8,128)(2,1)S(1)}, u32[]{:S(2)}, u32[]{:S(2)}) collective-permute-start(s16[4,16,1920]{2,1,0:T(8,128)(2,1)S(1)} %pad_add_fusion.near_ref), channel_id=1, source_target_pairs={{0,4},{4,0},{8,12},{12,8},{16,20},{20,16},{24,28},{28,24},{1,5},{5... | collective-permute-start | bytes 737288 | tf_op jit(solution)/shard_map/ppermute | solution.py:433
  90.0 5.1 %copy-start = (f32[1024,512]{1,0:T(8,128)S(1)}, f32[1024,512]{1,0:T(8,128)}, u32[]{:S(2)}) copy-start(f32[1024,512]{1,0:T(8,128)} %get-tuple-element.13.a_ref) | copy-start | bytes 6291460

commit v2 on v1

--- a/solution.py
+++ b/solution.py
@@ -321,10 +321,10 @@
     )(a, b, code)
 
 
-def update_kernel(places, per_owner, chained, ids_ref, near_ref, far_ref, freq_ref, ct_ref, *refs):
+def update_kernel(places, per_owner, chained, ids_ref, me_ref, near_ref, far_ref, freq_ref, ct_ref, *refs):
     if chained:
         refs = refs[1:]
-    out_ref, held_ref, out_buf, out_sem = refs
+    out_ref, held_ref, lanes_ref, out_buf, out_sem = refs
     steps = len(places)
     rows = steps * PER_STEP
     hidden = out_ref.shape[1]
@@ -333,13 +333,24 @@
     for side, ref in enumerate((near_ref, far_ref)):
         for slot in range(total):
             values = decode_rows(ref[slot])
-            start = pl.multiple_of((ids_ref[1] ^ (2 * slot + side)) * rows, 8)
+            start = pl.multiple_of((me_ref[0] ^ (2 * slot + side)) * rows, 8)
             for strip in range(hidden // LANES):
                 held_ref[strip, pl.ds(start, rows), :] = values[:, strip * LANES : (strip + 1) * LANES]
 
     groups = hidden // (4 * TILE)
     wide = groups * LANES
-    number = lax.broadcasted_iota(jnp.int32, (TILE, wide), 0)
+    packed, tile_rows = freq_ref.shape
+    short = 4 * replicas
+    source = lax.broadcasted_iota(jnp.int32, (packed, wide), 0)
+    target = lax.broadcasted_iota(jnp.int32, (packed, wide), 1)
+    same = (source // short == target // LANES) & (source % short == target % short)
+    lanes_ref[:tile_rows] = lax.dot_general(
+        freq_ref[...].astype(jnp.float32).astype(jnp.bfloat16),
+        same.astype(jnp.float32).astype(jnp.bfloat16),
+        (((0,), (0,)), ((), ())),
+        preferred_element_type=jnp.float32,
+    )
+    number = lax.broadcasted_iota(jnp.int32, (TILE, wide), 0).astype(jnp.float32)
     main = (lax.broadcasted_iota(jnp.int32, (TILE, wide), 1) % LANES) < TILE
     lane_tile = lax.broadcasted_iota(jnp.int32, (replicas, 4 * TILE), 1) // TILE
 
@@ -347,7 +358,7 @@
         block = block_of(ids_ref, places[step], per_owner)
 
         def tile_row(tr, carry):
-            onehot = number == freq_ref[pl.ds(block * PER_STEP + tr, 1), :]
+            onehot = number == lanes_ref[pl.ds(block * PER_STEP + tr, 1), :]
             onehot = onehot.astype(jnp.float32).astype(jnp.bfloat16)
             columns = jnp.dot(
                 ct_ref[...],
@@ -384,18 +395,18 @@
         pltpu.make_async_copy(out_buf.at[step], target, out_sem.at[step]).wait()
 
 
-def update_call(places, ids, near, far, freq_lanes, features, per_owner, chained):
+def update_call(places, ids, me, near, far, freq_lanes, features, per_owner, chained):
     hidden = near.shape[2] - LANES
     steps = len(places)
     rows = steps * PER_STEP
     anywhere = pl.BlockSpec(memory_space=pltpu.HBM)
     table = jnp.concatenate(split3(cosine_constant().T), axis=1)
-    operands = [ids, near, far, freq_lanes, table]
+    operands = [ids, me, near, far, freq_lanes, table]
     in_specs = [
-        pl.BlockSpec(near.shape, lambda i, ids: (0, 0, 0)),
-        pl.BlockSpec(far.shape, lambda i, ids: (0, 0, 0)),
-        pl.BlockSpec(freq_lanes.shape, lambda i, ids: (0, 0)),
-        pl.BlockSpec(table.shape, lambda i, ids: (0, 0)),
+        pl.BlockSpec(near.shape, lambda i, ids, me: (0, 0, 0)),
+        pl.BlockSpec(far.shape, lambda i, ids, me: (0, 0, 0)),
+        pl.BlockSpec(freq_lanes.shape, lambda i, ids, me: (0, 0)),
+        pl.BlockSpec(table.shape, lambda i, ids, me: (0, 0)),
     ]
     aliases = {}
     if chained is not None:
@@ -406,12 +417,13 @@
     return pl.pallas_call(
         functools.partial(update_kernel, places, per_owner, chained is not None),
         grid_spec=pltpu.PrefetchScalarGridSpec(
-            num_scalar_prefetch=1,
+            num_scalar_prefetch=2,
             grid=(1,),
             in_specs=in_specs,
             out_specs=anywhere,
             scratch_shapes=[
                 pltpu.VMEM((hidden // LANES, (replicas + 1) * rows, LANES), jnp.float32),
+                pltpu.VMEM((freq_lanes.shape[1] + PAD, hidden // STRIP * LANES), jnp.float32),
                 pltpu.VMEM((steps, STEP, hidden), jnp.bfloat16),
                 pltpu.SemaphoreType.DMA((steps,)),
             ],
@@ -440,7 +452,7 @@
 def fast_layer(activations, grad_out, weight, momentum, freq_rows):
     device = lax.axis_index("tensor")
     replica = lax.axis_index("replica")
-    ids = jnp.stack([device, replica])
+    ids, me = device[None], replica[None]
     features, _ = weight.shape
     width = activations.shape[1]
     per_owner = width // STEP
@@ -454,13 +466,8 @@
 
     for_twin, for_far = partial_call((3, 2), ids, grad_out, weight, width)
     received = flip(for_twin, "tensor", 1)
-    lanes = freq_rows.reshape(replicas, tile_rows, tile_cols // 4, 1, 4)
-    lanes = jnp.transpose(lanes, (1, 2, 3, 4, 0))
-    lanes = jnp.broadcast_to(lanes, (tile_rows, tile_cols // 4, 4, 4, replicas))
-    lanes = lanes.reshape(tile_rows, tile_cols // 4 * 16 * replicas)
-    lanes = jnp.pad(lanes, ((0, PAD), (0, 0)))
     chosen = lax.dynamic_index_in_dim(freq_rows, replica, 0, keepdims=False)
-    received, lanes = lax.optimization_barrier((received, lanes))
+    lanes = jnp.transpose(freq_rows, (2, 0, 1)).reshape(tile_cols * replicas, tile_rows)
     code = add_encode(for_far, received, 2)
     code = flip(code, "tensor", 2)
     for_twin, own = partial_call((1, 0), ids, grad_out, weight, width)
@@ -480,7 +487,7 @@
     for half in range(2):
         near = jnp.stack([codes[half]] + [flip(codes[half], "replica", mask) for mask in range(2, replicas, 2)])
         far = flip(near, "replica", 1)
-        update = update_call(places[half], ids, near, far, lanes, features, per_owner, update)
+        update = update_call(places[half], ids, me, near, far, lanes, features, per_owner, update)
 
     input_grad = add_decode(own, own_twin, code, 2)
     return (input_grad, out[None], update)

time: 96.6 us -> 91.9 us (0.951)
  Pallas kernels: 53.6 us -> 50.4 us
  local copies, waits for them, and re-layouts: 2.15 us -> 0.12 us
  waiting for transfers between devices: 21.2 us -> 22.5 us
    pallas_call x2, Pallas kernels: 16.4 us -> 15 us  [partial_call(): pl.pallas_call(functools.partial(partial_kernel, masks), grid_spec=pltpu....]
    ppermute x14, waiting for transfers between devices: 21.2 us -> 22.5 us  [flip(): return lax.ppermute(x, axis, [(i, i ^ mask) for i in range(size)])]
    reshape x1 -> x0, local copies, waits for them, and re-layouts: 1.18 us -> none  [fast_layer(): lanes = lanes.reshape(tile_rows, tile_cols // 4 * 16 * replicas)]
  transfers between devices with their start and end apart: 14 -> 14, of which waited for: 4 -> 4; matrix products, arithmetic and copies ran while one was open for 3% -> 0% of each run, Pallas kernels for 54% -> 54%
where the time goes in v2:
time: 91.9 us; the launch traced here: 91.8 us
  Pallas kernels  50.4 us (55%)
  waiting for transfers between devices  22.5 us (24%)
  starting transfers between devices  18 us (20%)
    pallas_call x2, Pallas kernels, grad_call(): pl.pallas_call(functools.partial(grad_kernel, len(acts), places, per_owne...  22.9 us
    ppermute x14, waiting for transfers between devices, flip(): return lax.ppermute(x, axis, [(i, i ^ mask) for i in range(size)])  22.5 us
    ppermute x14, starting transfers between devices, flip(): return lax.ppermute(x, axis, [(i, i ^ mask) for i in range(size)])  18 us
    pallas_call x2, Pallas kernels, partial_call(): pl.pallas_call(functools.partial(partial_kernel, masks), grid_spec=pltpu....  15 us
    pallas_call x2, Pallas kernels, update_call(): pl.pallas_call(functools.partial(update_kernel, places, per_owner, chaine...  9.15 us
    pallas_call x1, Pallas kernels, add_encode(): pl.pallas_call(add_encode_kernel, grid=(blocks,), in_specs=[spec, spec],...  2.07 us
  transfers between devices with their start and end apart: 14, of which 4 were waited for; matrix products, arithmetic and copies ran while one was open for 0% of the time, Pallas kernels for 54%

profile of v2, /device:TPU:0, one launch (start us, length us, event | category | flops | bytes accessed | tf_op | source)
XLA Modules:
  0.0 91.8 jit_solution(5713439276093164023)
XLA Ops:
  0.6 3.0 %collective-permute-start.3 = (bf16[1024,512]{1,0:T(8,128)(2,1)}, bf16[1024,512]{1,0:T(8,128)(2,1)}, u32[]{:S(2)}, u32[]{:S(2)}) collective-permute-start(bf16[1024,512]{1,0:T(8,128)(2,1)} %refs_2_.1), channel_id=1, source_target_pairs={{0,2},{1,3},{2,0},{3,1},{4,6},{5,7},{6,4},{7,5},{8,10},{9,11},{10,... | collective-permute-start | bytes 3145736 | tf_op jit(solution)/shard_map/ppermute | solution.py:445
  3.7 0.0 copy-start.2
  3.7 7.6 %partial_products.3 = (f32[1024,512]{1,0:T(8,128)}, f32[1024,512]{1,0:T(8,128)}) custom-call(s32[1]{0:T(128)} %bitcast.ids_ref.refs_0_, bf16[1024,1792]{1,0:T(8,128)(2,1)} %refs_4_.3, bf16[2048,1792]{1,0:T(8,128)(2,1)} %w_ref.3), custom_call_target="tpu_custom_call" | custom-call | flops 3758096384 | bytes 11534336 | tf_op jit(solution)/shard_map/partial_products/pallas_call | solution.py:249
  11.2 0.0 copy-start.3
  11.3 0.0 copy-start.5
  11.3 0.1 collective-permute-start.1
  11.4 0.0 copy-done.2
  11.4 0.5 collective-permute-start.5
  11.8 15.3 %collective-permute-done.3.refs_2_ = bf16[1024,512]{1,0:T(8,128)(2,1)} collective-permute-done((bf16[1024,512]{1,0:T(8,128)(2,1)}, bf16[1024,512]{1,0:T(8,128)(2,1)}, u32[]{:S(2)}, u32[]{:S(2)}) %collective-permute-start.3) | collective-permute-done | bytes 1048608 | tf_op jit(solution)/shard_map/ppermute | solution.py:445
  27.1 0.0 collective-permute-start.4
  27.1 7.5 %partial_products.2 = (f32[1024,512]{1,0:T(8,128)}, f32[1024,512]{1,0:T(8,128)}) custom-call(s32[1]{0:T(128)} %bitcast.ids_ref.refs_0_, bf16[1024,1792]{1,0:T(8,128)(2,1)} %refs_4_.3, bf16[2048,1792]{1,0:T(8,128)(2,1)} %w_ref.3), custom_call_target="tpu_custom_call" | custom-call | flops 3758096384 | bytes 11534336 | tf_op jit(solution)/shard_map/partial_products/pallas_call | solution.py:249
  34.6 0.6 collective-permute-start
  35.2 0.0 copy-done.3
  35.2 0.1 copy.18
  35.3 0.0 collective-permute-done.5.refs_3_
  35.3 0.0 copy-done.5
  35.3 0.0 copy-start.1
  35.3 11.4 %grad_step.2 = (f32[2048,1792]{1,0:T(8,128)}, s16[16,1920]{1,0:T(8,128)(2,1)S(1)}) custom-call(s32[1]{0:T(128)} %bitcast.ids_ref.refs_0_, s32[32,28]{1,0:T(8,128)S(1)} %bitcast.18, bf16[1024,512]{1,0:T(8,128)(2,1)S(1)} %copy-done.2, bf16[1024,512]{1,0:T(8,128)(2,1)} %collective-permute-done.5.refs_3_, bf16[1024,1792]{1,0:T(8,128)(2,1)} %refs_4_.3, ...), custom_call_target="tpu_custom_call" | custom-call | flops 3758096384 | bytes 18350080 | tf_op jit(solution)/shard_map/grad_step/pallas_call | solution.py:177
  46.7 3.9 %collective-permute-start.12 = (s16[16,1920]{1,0:T(8,128)(2,1)S(1)}, s16[16,1920]{1,0:T(8,128)(2,1)S(1)}, u32[]{:S(2)}, u32[]{:S(2)}) collective-permute-start(s16[16,1920]{1,0:T(8,128)(2,1)S(1)} %get-tuple-element.18), channel_id=1, source_target_pairs={{0,24},{4,28},{8,16},{12,20},{16,8},{20,12},{24,0},{28,4},{1,25},{... | collective-permute-start | bytes 184328 | tf_op jit(solution)/shard_map/ppermute | solution.py:445
  50.6 0.0 collective-permute-start.11
  50.6 0.0 collective-permute-done.1.b_ref
  50.6 0.6 collective-permute-start.10
  51.3 0.0 copy-done.1
  51.3 2.1 %add_encode.1 = s16[1056,512]{1,0:T(8,128)(2,1)S(1)} custom-call(f32[1024,512]{1,0:T(8,128)S(1)} %copy-done.1, f32[1024,512]{1,0:T(8,128)} %collective-permute-done.1.b_ref), custom_call_target="tpu_custom_call" | custom-call | flops 4194304 | bytes 5242880 | tf_op jit(solution)/shard_map/add_encode/pallas_call | solution.py:289
  53.3 0.0 collective-permute-done.4.refs_3_
  53.4 1.7 %collective-permute-start.2 = (s16[1056,512]{1,0:T(8,128)(2,1)S(1)}, s16[1056,512]{1,0:T(8,128)(2,1)S(1)}, u32[]{:S(2)}, u32[]{:S(2)}) collective-permute-start(s16[1056,512]{1,0:T(8,128)(2,1)S(1)} %add_encode.1), channel_id=1, source_target_pairs={{0,2},{1,3},{2,0},{3,1},{4,6},{5,7},{6,4},{7,5},{8,10},{9,11},{10,... | collective-permute-start | bytes 3244040 | tf_op jit(solution)/shard_map/ppermute | solution.py:445
  55.1 11.5 %grad_step.3 = (f32[2048,1792]{1,0:T(8,128)}, s16[16,1920]{1,0:T(8,128)(2,1)S(1)}) custom-call(s32[1]{0:T(128)} %bitcast.ids_ref.refs_0_, s32[32,28]{1,0:T(8,128)S(1)} %bitcast.19, bf16[1024,512]{1,0:T(8,128)(2,1)} %collective-permute-done.3.refs_2_, bf16[1024,512]{1,0:T(8,128)(2,1)} %collective-permute-done.4.refs_3_, ...), custom_call_target="tpu_custom_call", output_to_operand_aliasing={{0}: (7, {})} | custom-call | flops 3758096384 | bytes 18350080 | tf_op jit(solution)/shard_map/grad_step/pallas_call | solution.py:177
  66.5 0.0 collective-permute-done.12
  66.6 3.7 %collective-permute-start.8 = (s16[16,1920]{1,0:T(8,128)(2,1)S(1)}, s16[16,1920]{1,0:T(8,128)(2,1)S(1)}, u32[]{:S(2)}, u32[]{:S(2)}) collective-permute-start(s16[16,1920]{1,0:T(8,128)(2,1)S(1)} %get-tuple-element.17), channel_id=1, source_target_pairs={{0,24},{4,28},{8,16},{12,20},{16,8},{20,12},{24,0},{28,4},{1,25},{... | collective-permute-start | bytes 184328 | tf_op jit(solution)/shard_map/ppermute | solution.py:445
  70.2 0.0 collective-permute-done.11
  70.2 0.0 collective-permute-start.7
  70.2 0.0 collective-permute-done.10
  70.2 0.8 collective-permute-start.6
  71.0 1.7 %collective-permute-done.8 = s16[16,1920]{1,0:T(8,128)(2,1)S(1)} collective-permute-done((s16[16,1920]{1,0:T(8,128)(2,1)S(1)}, s16[16,1920]{1,0:T(8,128)(2,1)S(1)}, u32[]{:S(2)}, u32[]{:S(2)}) %collective-permute-start.8) | collective-permute-done | bytes 61472 | tf_op jit(solution)/shard_map/ppermute | solution.py:445
  72.8 1.5 %collective-permute-start.13 = (s16[4,16,1920]{2,1,0:T(8,128)(2,1)S(1)}, s16[4,16,1920]{2,1,0:T(8,128)(2,1)S(1)}, u32[]{:S(2)}, u32[]{:S(2)}) collective-permute-start(s16[4,16,1920]{2,1,0:T(8,128)(2,1)S(1)} %pad_add_fusion.1.near_ref), channel_id=1, source_target_pairs={{0,4},{4,0},{8,12},{12,8},{16,20},{20,16},{24,28},{28,24},{1,5},{5... | collective-permute-start | bytes 737288 | tf_op jit(solution)/shard_map/ppermute | solution.py:445
  74.3 1.1 %collective-permute-done.7 = s16[16,1920]{1,0:T(8,128)(2,1)S(1)} collective-permute-done((s16[16,1920]{1,0:T(8,128)(2,1)S(1)}, s16[16,1920]{1,0:T(8,128)(2,1)S(1)}, u32[]{:S(2)}, u32[]{:S(2)}) %collective-permute-start.7) | collective-permute-done | bytes 61472 | tf_op jit(solution)/shard_map/ppermute | solution.py:445
  75.3 0.0 collective-permute-done.6
  75.4 1.6 %collective-permute-start.9 = (s16[4,16,1920]{2,1,0:T(8,128)(2,1)S(1)}, s16[4,16,1920]{2,1,0:T(8,128)(2,1)S(1)}, u32[]{:S(2)}, u32[]{:S(2)}) collective-permute-start(s16[4,16,1920]{2,1,0:T(8,128)(2,1)S(1)} %pad_add_fusion.near_ref), channel_id=1, source_target_pairs={{0,4},{4,0},{8,12},{12,8},{16,20},{20,16},{24,28},{28,24},{1,5},{5... | collective-permute-start | bytes 737288 | tf_op jit(solution)/shard_map/ppermute | solution.py:445
  77.0 4.4 %collective-permute-done.13.far_ref = s16[4,16,1920]{2,1,0:T(8,128)(2,1)S(1)} collective-permute-done((s16[4,16,1920]{2,1,0:T(8,128)(2,1)S(1)}, s16[4,16,1920]{2,1,0:T(8,128)(2,1)S(1)}, u32[]{:S(2)}, u32[]{:S(2)}) %collective-permute-start.13) | collective-permute-done | bytes 245792 | tf_op jit(solution)/shard_map/ppermute | solution.py:445
  81.3 0.0 copy-done.4
  81.3 4.6 %update_rows.2.refs_0_ = bf16[2048,1792]{1,0:T(8,128)(2,1)} custom-call(s32[1]{0:T(128)} %bitcast.ids_ref.refs_0_, s32[1]{0:T(128)} %bitcast.4.me_ref, s16[4,16,1920]{2,1,0:T(8,128)(2,1)S(1)} %pad_add_fusion.1.near_ref, s16[4,16,1920]{2,1,0:T(8,128)(2,1)S(1)} %collective-permute-done.13.far_ref, s32[224,32]{1,0:T(8,128)S(1)} %bitcast.16, ...), custom_call_target="tpu_custom_call" | custom-call | flops 1879048192 | bytes 3670016 | tf_op jit(solution)/shard_map/update_rows/pallas_call | solution.py:417
  85.9 0.0 copy-start
  85.9 0.0 collective-permute-done.9.far_ref
  85.9 4.6 %update_rows.3 = bf16[2048,1792]{1,0:T(8,128)(2,1)} custom-call(s32[1]{0:T(128)} %bitcast.ids_ref.refs_0_, s32[1]{0:T(128)} %bitcast.4.me_ref, s16[4,16,1920]{2,1,0:T(8,128)(2,1)S(1)} %pad_add_fusion.near_ref, s16[4,16,1920]{2,1,0:T(8,128)(2,1)S(1)} %collective-permute-done.9.far_ref, s32[224,32]{1,0:T(8,128)S(1)} %bitcast.17, ...), custom_call_target="tpu_custom_call", output_to_operand_aliasing={{}: (6, {})} | custom-call | flops 1879048192 | bytes 3670016 | tf_op jit(solution)/shard_map/update_rows/pallas_call | solution.py:417
  90.5 0.0 collective-permute-done.b_ref
  90.5 0.0 collective-permute-done.2.code_ref
  90.6 0.0 copy-done
  90.6 1.2 %add_decode.1 = bf16[1024,512]{1,0:T(8,128)(2,1)} custom-call(f32[1024,512]{1,0:T(8,128)S(1)} %copy-done, f32[1024,512]{1,0:T(8,128)S(1)} %collective-permute-done.b_ref, s16[1056,512]{1,0:T(8,128)(2,1)S(1)} %collective-permute-done.2.code_ref), custom_call_target="tpu_custom_call" | custom-call | flops 4194304 | bytes 6291456 | tf_op jit(solution)/shard_map/add_decode/pallas_call | solution.py:312
  (4 shorter events, 0.1 us)
Async XLA Ops:
  0.6 26.5 %collective-permute-start.3 = (bf16[1024,512]{1,0:T(8,128)(2,1)}, bf16[1024,512]{1,0:T(8,128)(2,1)}, u32[]{:S(2)}, u32[]{:S(2)}) collective-permute-start(bf16[1024,512]{1,0:T(8,128)(2,1)} %refs_2_.1), channel_id=1, source_target_pairs={{0,2},{1,3},{2,0},{3,1},{4,6},{5,7},{6,4},{7,5},{8,10},{9,11},{10,... | collective-permute-start | bytes 3145736 | tf_op jit(solution)/shard_map/ppermute | solution.py:445
  3.7 7.7 %copy-start.2 = (bf16[1024,512]{1,0:T(8,128)(2,1)S(1)}, bf16[1024,512]{1,0:T(8,128)(2,1)}, u32[]{:S(2)}) copy-start(bf16[1024,512]{1,0:T(8,128)(2,1)} %refs_2_.1) | copy-start | bytes 3145732
  11.2 23.9 %copy-start.3 = (s32[8,32,28]{1,0,2:T(8,128)S(1)}, s32[8,32,28]{1,0,2:T(8,128)}, u32[]{:S(2)}) copy-start(s32[8,32,28]{1,0,2:T(8,128)} %param.17) | copy-start | bytes 86020
  11.3 24.0 %copy-start.5 = (f32[64,64]{1,0:T(8,128)S(1)}, f32[64,64]{1,0:T(8,128)}, u32[]{:S(2)}) copy-start(f32[64,64]{1,0:T(8,128)} %constant.23.clone.refs_6_) | copy-start | bytes 49156
  11.3 39.3 %collective-permute-start.1 = (f32[1024,512]{1,0:T(8,128)}, f32[1024,512]{1,0:T(8,128)}, u32[]{:S(2)}, u32[]{:S(2)}) collective-permute-start(f32[1024,512]{1,0:T(8,128)} %get-tuple-element.14), channel_id=1, source_target_pairs={{0,1},{1,0},{2,3},{3,2},{4,5},{5,4},{6,7},{7,6},{8,9},{9,8},{10,11... | collective-permute-start | bytes 6291464 | tf_op jit(solution)/shard_map/ppermute | solution.py:445
  11.4 23.9 %collective-permute-start.5 = (bf16[1024,512]{1,0:T(8,128)(2,1)S(1)}, bf16[1024,512]{1,0:T(8,128)(2,1)}, u32[]{:S(2)}, u32[]{:S(2)}) collective-permute-start(bf16[1024,512]{1,0:T(8,128)(2,1)S(1)} %copy-done.2), channel_id=1, source_target_pairs={{0,1},{1,0},{2,3},{3,2},{4,5},{5,4},{6,7},{7,6},{8,9},{9,8},{10,11... | collective-permute-start | bytes 3145736 | tf_op jit(solution)/shard_map/ppermute | solution.py:445
  27.1 26.2 %collective-permute-start.4 = (bf16[1024,512]{1,0:T(8,128)(2,1)}, bf16[1024,512]{1,0:T(8,128)(2,1)}, u32[]{:S(2)}, u32[]{:S(2)}) collective-permute-start(bf16[1024,512]{1,0:T(8,128)(2,1)} %collective-permute-done.3.refs_2_), channel_id=1, source_target_pairs={{0,1},{1,0},{2,3},{3,2},{4,5},{5,4},{6,7},{7,6},{8,9},{9,8},{10,11... | collective-permute-start | bytes 3145736 | tf_op jit(solution)/shard_map/ppermute | solution.py:445
  34.6 55.9 %collective-permute-start = (f32[1024,512]{1,0:T(8,128)}, f32[1024,512]{1,0:T(8,128)S(1)}, u32[]{:S(2)}, u32[]{:S(2)}) collective-permute-start(f32[1024,512]{1,0:T(8,128)} %get-tuple-element.12), channel_id=1, source_target_pairs={{0,1},{1,0},{2,3},{3,2},{4,5},{5,4},{6,7},{7,6},{8,9},{9,8},{10,11... | collective-permute-start | bytes 6291464 | tf_op jit(solution)/shard_map/ppermute | solution.py:445
  35.3 16.0 %copy-start.1 = (f32[1024,512]{1,0:T(8,128)S(1)}, f32[1024,512]{1,0:T(8,128)}, u32[]{:S(2)}) copy-start(f32[1024,512]{1,0:T(8,128)} %get-tuple-element.13.a_ref) | copy-start | bytes 6291460
  46.7 19.9 %collective-permute-start.12 = (s16[16,1920]{1,0:T(8,128)(2,1)S(1)}, s16[16,1920]{1,0:T(8,128)(2,1)S(1)}, u32[]{:S(2)}, u32[]{:S(2)}) collective-permute-start(s16[16,1920]{1,0:T(8,128)(2,1)S(1)} %get-tuple-element.18), channel_id=1, source_target_pairs={{0,24},{4,28},{8,16},{12,20},{16,8},{20,12},{24,0},{28,4},{1,25},{... | collective-permute-start | bytes 184328 | tf_op jit(solution)/shard_map/ppermute | solution.py:445
  50.6 19.6 %collective-permute-start.11 = (s16[16,1920]{1,0:T(8,128)(2,1)S(1)}, s16[16,1920]{1,0:T(8,128)(2,1)S(1)}, u32[]{:S(2)}, u32[]{:S(2)}) collective-permute-start(s16[16,1920]{1,0:T(8,128)(2,1)S(1)} %get-tuple-element.18), channel_id=1, source_target_pairs={{0,16},{4,20},{8,24},{12,28},{16,0},{20,4},{24,8},{28,12},{1,17},{... | collective-permute-start | bytes 184328 | tf_op jit(solution)/shard_map/ppermute | solution.py:445
  50.6 19.6 %collective-permute-start.10 = (s16[16,1920]{1,0:T(8,128)(2,1)S(1)}, s16[16,1920]{1,0:T(8,128)(2,1)S(1)}, u32[]{:S(2)}, u32[]{:S(2)}) collective-permute-start(s16[16,1920]{1,0:T(8,128)(2,1)S(1)} %get-tuple-element.18), channel_id=1, source_target_pairs={{0,8},{4,12},{8,0},{12,4},{16,24},{20,28},{24,16},{28,20},{1,9},{5... | collective-permute-start | bytes 184328 | tf_op jit(solution)/shard_map/ppermute | solution.py:445
  53.4 37.2 %collective-permute-start.2 = (s16[1056,512]{1,0:T(8,128)(2,1)S(1)}, s16[1056,512]{1,0:T(8,128)(2,1)S(1)}, u32[]{:S(2)}, u32[]{:S(2)}) collective-permute-start(s16[1056,512]{1,0:T(8,128)(2,1)S(1)} %add_encode.1), channel_id=1, source_target_pairs={{0,2},{1,3},{2,0},{3,1},{4,6},{5,7},{6,4},{7,5},{8,10},{9,11},{10,... | collective-permute-start | bytes 3244040 | tf_op jit(solution)/shard_map/ppermute | solution.py:445
  55.1 26.3 %copy-start.4 = (bf16[64,192]{1,0:T(8,128)(2,1)S(1)}, bf16[64,192]{1,0:T(8,128)(2,1)}, u32[]{:S(2)}) copy-start(bf16[64,192]{1,0:T(8,128)(2,1)} %constant.28.ct_ref) | copy-start | bytes 73732
  66.6 6.2 %collective-permute-start.8 = (s16[16,1920]{1,0:T(8,128)(2,1)S(1)}, s16[16,1920]{1,0:T(8,128)(2,1)S(1)}, u32[]{:S(2)}, u32[]{:S(2)}) collective-permute-start(s16[16,1920]{1,0:T(8,128)(2,1)S(1)} %get-tuple-element.17), channel_id=1, source_target_pairs={{0,24},{4,28},{8,16},{12,20},{16,8},{20,12},{24,0},{28,4},{1,25},{... | collective-permute-start | bytes 184328 | tf_op jit(solution)/shard_map/ppermute | solution.py:445
  70.2 5.1 %collective-permute-start.7 = (s16[16,1920]{1,0:T(8,128)(2,1)S(1)}, s16[16,1920]{1,0:T(8,128)(2,1)S(1)}, u32[]{:S(2)}, u32[]{:S(2)}) collective-permute-start(s16[16,1920]{1,0:T(8,128)(2,1)S(1)} %get-tuple-element.17), channel_id=1, source_target_pairs={{0,16},{4,20},{8,24},{12,28},{16,0},{20,4},{24,8},{28,12},{1,17},{... | collective-permute-start | bytes 184328 | tf_op jit(solution)/shard_map/ppermute | solution.py:445
  70.2 5.1 %collective-permute-start.6 = (s16[16,1920]{1,0:T(8,128)(2,1)S(1)}, s16[16,1920]{1,0:T(8,128)(2,1)S(1)}, u32[]{:S(2)}, u32[]{:S(2)}) collective-permute-start(s16[16,1920]{1,0:T(8,128)(2,1)S(1)} %get-tuple-element.17), channel_id=1, source_target_pairs={{0,8},{4,12},{8,0},{12,4},{16,24},{20,28},{24,16},{28,20},{1,9},{5... | collective-permute-start | bytes 184328 | tf_op jit(solution)/shard_map/ppermute | solution.py:445
  72.8 8.6 %collective-permute-start.13 = (s16[4,16,1920]{2,1,0:T(8,128)(2,1)S(1)}, s16[4,16,1920]{2,1,0:T(8,128)(2,1)S(1)}, u32[]{:S(2)}, u32[]{:S(2)}) collective-permute-start(s16[4,16,1920]{2,1,0:T(8,128)(2,1)S(1)} %pad_add_fusion.1.near_ref), channel_id=1, source_target_pairs={{0,4},{4,0},{8,12},{12,8},{16,20},{20,16},{24,28},{28,24},{1,5},{5... | collective-permute-start | bytes 737288 | tf_op jit(solution)/shard_map/ppermute | solution.py:445
  75.4 10.6 %collective-permute-start.9 = (s16[4,16,1920]{2,1,0:T(8,128)(2,1)S(1)}, s16[4,16,1920]{2,1,0:T(8,128)(2,1)S(1)}, u32[]{:S(2)}, u32[]{:S(2)}) collective-permute-start(s16[4,16,1920]{2,1,0:T(8,128)(2,1)S(1)} %pad_add_fusion.near_ref), channel_id=1, source_target_pairs={{0,4},{4,0},{8,12},{12,8},{16,20},{20,16},{24,28},{28,24},{1,5},{5... | collective-permute-start | bytes 737288 | tf_op jit(solution)/shard_map/ppermute | solution.py:445
  85.9 4.6 %copy-start = (f32[1024,512]{1,0:T(8,128)S(1)}, f32[1024,512]{1,0:T(8,128)}, u32[]{:S(2)}) copy-start(f32[1024,512]{1,0:T(8,128)} %get-tuple-element.11.a_ref) | copy-start | bytes 6291460

commit v3 on v2

--- a/solution.py
+++ b/solution.py
@@ -213,7 +213,7 @@
 
 def partial_kernel(masks, ids_ref, go_ref, w_ref, *refs):
     out_refs, (go_buf, w_buf, out_buf, in_sem, out_sem) = refs[: len(masks)], refs[len(masks) :]
-    chunks, rows, _ = go_buf.shape
+    chunks, rows, hidden = go_buf.shape
     width = w_buf.shape[1]
     copies = []
     for n, mask in enumerate(masks):
@@ -225,14 +225,18 @@
     for n in (0, len(masks), *range(1, len(masks)), *range(len(masks) + 1, len(copies))):
         copies[n].start()
     outs = []
+    for m in range(len(masks)):
+        copies[m].wait()
     for n in range(chunks):
         copies[len(masks) + n].wait()
+        product = lax.dot_general(
+            go_buf[n],
+            w_buf[...].reshape(len(masks) * width, hidden),
+            (((1,), (1,)), ((), ())),
+            preferred_element_type=jnp.float32,
+        )
         for m in range(len(masks)):
-            if n == 0:
-                copies[m].wait()
-            out_buf[m, n] = lax.dot_general(
-                go_buf[n], w_buf[m], (((1,), (1,)), ((), ())), preferred_element_type=jnp.float32
-            )
+            out_buf[m, n] = product[:, m * width : (m + 1) * width]
             target = out_refs[m].at[pl.ds(n * rows, rows), :]
             outs.append(pltpu.make_async_copy(out_buf.at[m, n], target, out_sem.at[m, n]))
             outs[-1].start()

time: 91.9 us -> 92.3 us (level)
  no operation moved by 1% of the time
where the time goes in v3:
time: 92.3 us; the launch traced here: 92.1 us
  Pallas kernels  51.1 us (55%)
  waiting for transfers between devices  22.1 us (24%)
  starting transfers between devices  18 us (20%)
    pallas_call x2, Pallas kernels, grad_call(): pl.pallas_call(functools.partial(grad_kernel, len(acts), places, per_owne...  22.9 us
    ppermute x14, waiting for transfers between devices, flip(): return lax.ppermute(x, axis, [(i, i ^ mask) for i in range(size)])  22.1 us
    ppermute x14, starting transfers between devices, flip(): return lax.ppermute(x, axis, [(i, i ^ mask) for i in range(size)])  18 us
    pallas_call x2, Pallas kernels, partial_call(): pl.pallas_call(functools.partial(partial_kernel, masks), grid_spec=pltpu....  15.7 us
    pallas_call x2, Pallas kernels, update_call(): pl.pallas_call(functools.partial(update_kernel, places, per_owner, chaine...  9.15 us
    pallas_call x1, Pallas kernels, add_encode(): pl.pallas_call(add_encode_kernel, grid=(blocks,), in_specs=[spec, spec],...  2.07 us
  transfers between devices with their start and end apart: 14, of which 4 were waited for; matrix products, arithmetic and copies ran while one was open for 0% of the time, Pallas kernels for 54%

profile of v3, /device:TPU:0, one launch (start us, length us, event | category | flops | bytes accessed | tf_op | source)
XLA Modules:
  0.0 92.1 jit_solution(7279205326030743387)
XLA Ops:
  0.6 3.0 %collective-permute-start.3 = (bf16[1024,512]{1,0:T(8,128)(2,1)}, bf16[1024,512]{1,0:T(8,128)(2,1)}, u32[]{:S(2)}, u32[]{:S(2)}) collective-permute-start(bf16[1024,512]{1,0:T(8,128)(2,1)} %refs_2_.1), channel_id=1, source_target_pairs={{0,2},{1,3},{2,0},{3,1},{4,6},{5,7},{6,4},{7,5},{8,10},{9,11},{10,... | collective-permute-start | bytes 3145736 | tf_op jit(solution)/shard_map/ppermute | solution.py:449
  3.7 0.0 copy-start.2
  3.7 7.9 %partial_products.3 = (f32[1024,512]{1,0:T(8,128)}, f32[1024,512]{1,0:T(8,128)}) custom-call(s32[1]{0:T(128)} %bitcast.ids_ref.refs_0_, bf16[1024,1792]{1,0:T(8,128)(2,1)} %refs_4_.3, bf16[2048,1792]{1,0:T(8,128)(2,1)} %w_ref.3), custom_call_target="tpu_custom_call" | custom-call | flops 3758096384 | bytes 11534336 | tf_op jit(solution)/shard_map/partial_products/pallas_call | solution.py:253
  11.6 0.0 copy-start.3
  11.6 0.0 copy-start.5
  11.6 0.1 collective-permute-start.1
  11.7 0.0 copy-done.2
  11.7 0.5 collective-permute-start.5
  12.2 14.9 %collective-permute-done.3.refs_2_ = bf16[1024,512]{1,0:T(8,128)(2,1)} collective-permute-done((bf16[1024,512]{1,0:T(8,128)(2,1)}, bf16[1024,512]{1,0:T(8,128)(2,1)}, u32[]{:S(2)}, u32[]{:S(2)}) %collective-permute-start.3) | collective-permute-done | bytes 1048608 | tf_op jit(solution)/shard_map/ppermute | solution.py:449
  27.1 0.0 collective-permute-start.4
  27.1 7.8 %partial_products.2 = (f32[1024,512]{1,0:T(8,128)}, f32[1024,512]{1,0:T(8,128)}) custom-call(s32[1]{0:T(128)} %bitcast.ids_ref.refs_0_, bf16[1024,1792]{1,0:T(8,128)(2,1)} %refs_4_.3, bf16[2048,1792]{1,0:T(8,128)(2,1)} %w_ref.3), custom_call_target="tpu_custom_call" | custom-call | flops 3758096384 | bytes 11534336 | tf_op jit(solution)/shard_map/partial_products/pallas_call | solution.py:253
  35.0 0.6 collective-permute-start
  35.5 0.0 copy-done.3
  35.6 0.1 copy.18
  35.6 0.0 collective-permute-done.5.refs_3_
  35.6 0.0 copy-done.5
  35.6 0.0 copy-start.1
  35.7 11.4 %grad_step.2 = (f32[2048,1792]{1,0:T(8,128)}, s16[16,1920]{1,0:T(8,128)(2,1)S(1)}) custom-call(s32[1]{0:T(128)} %bitcast.ids_ref.refs_0_, s32[32,28]{1,0:T(8,128)S(1)} %bitcast.18, bf16[1024,512]{1,0:T(8,128)(2,1)S(1)} %copy-done.2, bf16[1024,512]{1,0:T(8,128)(2,1)} %collective-permute-done.5.refs_3_, bf16[1024,1792]{1,0:T(8,128)(2,1)} %refs_4_.3, ...), custom_call_target="tpu_custom_call" | custom-call | flops 3758096384 | bytes 18350080 | tf_op jit(solution)/shard_map/grad_step/pallas_call | solution.py:177
  47.0 3.9 %collective-permute-start.12 = (s16[16,1920]{1,0:T(8,128)(2,1)S(1)}, s16[16,1920]{1,0:T(8,128)(2,1)S(1)}, u32[]{:S(2)}, u32[]{:S(2)}) collective-permute-start(s16[16,1920]{1,0:T(8,128)(2,1)S(1)} %get-tuple-element.18), channel_id=1, source_target_pairs={{0,24},{4,28},{8,16},{12,20},{16,8},{20,12},{24,0},{28,4},{1,25},{... | collective-permute-start | bytes 184328 | tf_op jit(solution)/shard_map/ppermute | solution.py:449
  51.0 0.0 collective-permute-start.11
  51.0 0.0 collective-permute-done.1.b_ref
  51.0 0.6 collective-permute-start.10
  51.6 0.0 copy-done.1
  51.6 2.1 %add_encode.1 = s16[1056,512]{1,0:T(8,128)(2,1)S(1)} custom-call(f32[1024,512]{1,0:T(8,128)S(1)} %copy-done.1, f32[1024,512]{1,0:T(8,128)} %collective-permute-done.1.b_ref), custom_call_target="tpu_custom_call" | custom-call | flops 4194304 | bytes 5242880 | tf_op jit(solution)/shard_map/add_encode/pallas_call | solution.py:293
  53.7 0.0 collective-permute-done.4.refs_3_
  53.7 1.7 %collective-permute-start.2 = (s16[1056,512]{1,0:T(8,128)(2,1)S(1)}, s16[1056,512]{1,0:T(8,128)(2,1)S(1)}, u32[]{:S(2)}, u32[]{:S(2)}) collective-permute-start(s16[1056,512]{1,0:T(8,128)(2,1)S(1)} %add_encode.1), channel_id=1, source_target_pairs={{0,2},{1,3},{2,0},{3,1},{4,6},{5,7},{6,4},{7,5},{8,10},{9,11},{10,... | collective-permute-start | bytes 3244040 | tf_op jit(solution)/shard_map/ppermute | solution.py:449
  55.4 11.5 %grad_step.3 = (f32[2048,1792]{1,0:T(8,128)}, s16[16,1920]{1,0:T(8,128)(2,1)S(1)}) custom-call(s32[1]{0:T(128)} %bitcast.ids_ref.refs_0_, s32[32,28]{1,0:T(8,128)S(1)} %bitcast.19, bf16[1024,512]{1,0:T(8,128)(2,1)} %collective-permute-done.3.refs_2_, bf16[1024,512]{1,0:T(8,128)(2,1)} %collective-permute-done.4.refs_3_, ...), custom_call_target="tpu_custom_call", output_to_operand_aliasing={{0}: (7, {})} | custom-call | flops 3758096384 | bytes 18350080 | tf_op jit(solution)/shard_map/grad_step/pallas_call | solution.py:177
  66.9 0.0 collective-permute-done.12
  66.9 3.7 %collective-permute-start.8 = (s16[16,1920]{1,0:T(8,128)(2,1)S(1)}, s16[16,1920]{1,0:T(8,128)(2,1)S(1)}, u32[]{:S(2)}, u32[]{:S(2)}) collective-permute-start(s16[16,1920]{1,0:T(8,128)(2,1)S(1)} %get-tuple-element.17), channel_id=1, source_target_pairs={{0,24},{4,28},{8,16},{12,20},{16,8},{20,12},{24,0},{28,4},{1,25},{... | collective-permute-start | bytes 184328 | tf_op jit(solution)/shard_map/ppermute | solution.py:449
  70.6 0.0 collective-permute-done.11
  70.6 0.0 collective-permute-start.7
  70.6 0.0 collective-permute-done.10
  70.6 0.8 collective-permute-start.6
  71.4 1.7 %collective-permute-done.8 = s16[16,1920]{1,0:T(8,128)(2,1)S(1)} collective-permute-done((s16[16,1920]{1,0:T(8,128)(2,1)S(1)}, s16[16,1920]{1,0:T(8,128)(2,1)S(1)}, u32[]{:S(2)}, u32[]{:S(2)}) %collective-permute-start.8) | collective-permute-done | bytes 61472 | tf_op jit(solution)/shard_map/ppermute | solution.py:449
  73.1 1.5 %collective-permute-start.13 = (s16[4,16,1920]{2,1,0:T(8,128)(2,1)S(1)}, s16[4,16,1920]{2,1,0:T(8,128)(2,1)S(1)}, u32[]{:S(2)}, u32[]{:S(2)}) collective-permute-start(s16[4,16,1920]{2,1,0:T(8,128)(2,1)S(1)} %pad_add_fusion.1.near_ref), channel_id=1, source_target_pairs={{0,4},{4,0},{8,12},{12,8},{16,20},{20,16},{24,28},{28,24},{1,5},{5... | collective-permute-start | bytes 737288 | tf_op jit(solution)/shard_map/ppermute | solution.py:449
  74.6 1.1 %collective-permute-done.7 = s16[16,1920]{1,0:T(8,128)(2,1)S(1)} collective-permute-done((s16[16,1920]{1,0:T(8,128)(2,1)S(1)}, s16[16,1920]{1,0:T(8,128)(2,1)S(1)}, u32[]{:S(2)}, u32[]{:S(2)}) %collective-permute-start.7) | collective-permute-done | bytes 61472 | tf_op jit(solution)/shard_map/ppermute | solution.py:449
  75.7 0.0 collective-permute-done.6
  75.7 1.6 %collective-permute-start.9 = (s16[4,16,1920]{2,1,0:T(8,128)(2,1)S(1)}, s16[4,16,1920]{2,1,0:T(8,128)(2,1)S(1)}, u32[]{:S(2)}, u32[]{:S(2)}) collective-permute-start(s16[4,16,1920]{2,1,0:T(8,128)(2,1)S(1)} %pad_add_fusion.near_ref), channel_id=1, source_target_pairs={{0,4},{4,0},{8,12},{12,8},{16,20},{20,16},{24,28},{28,24},{1,5},{5... | collective-permute-start | bytes 737288 | tf_op jit(solution)/shard_map/ppermute | solution.py:449
  77.3 4.4 %collective-permute-done.13.far_ref = s16[4,16,1920]{2,1,0:T(8,128)(2,1)S(1)} collective-permute-done((s16[4,16,1920]{2,1,0:T(8,128)(2,1)S(1)}, s16[4,16,1920]{2,1,0:T(8,128)(2,1)S(1)}, u32[]{:S(2)}, u32[]{:S(2)}) %collective-permute-start.13) | collective-permute-done | bytes 245792 | tf_op jit(solution)/shard_map/ppermute | solution.py:449
  81.7 0.0 copy-done.4
  81.7 4.6 %update_rows.2.refs_0_ = bf16[2048,1792]{1,0:T(8,128)(2,1)} custom-call(s32[1]{0:T(128)} %bitcast.ids_ref.refs_0_, s32[1]{0:T(128)} %bitcast.4.me_ref, s16[4,16,1920]{2,1,0:T(8,128)(2,1)S(1)} %pad_add_fusion.1.near_ref, s16[4,16,1920]{2,1,0:T(8,128)(2,1)S(1)} %collective-permute-done.13.far_ref, s32[224,32]{1,0:T(8,128)S(1)} %bitcast.16, ...), custom_call_target="tpu_custom_call" | custom-call | flops 1879048192 | bytes 3670016 | tf_op jit(solution)/shard_map/update_rows/pallas_call | solution.py:421
  86.3 0.0 copy-start
  86.3 0.0 collective-permute-done.9.far_ref
  86.3 4.6 %update_rows.3 = bf16[2048,1792]{1,0:T(8,128)(2,1)} custom-call(s32[1]{0:T(128)} %bitcast.ids_ref.refs_0_, s32[1]{0:T(128)} %bitcast.4.me_ref, s16[4,16,1920]{2,1,0:T(8,128)(2,1)S(1)} %pad_add_fusion.near_ref, s16[4,16,1920]{2,1,0:T(8,128)(2,1)S(1)} %collective-permute-done.9.far_ref, s32[224,32]{1,0:T(8,128)S(1)} %bitcast.17, ...), custom_call_target="tpu_custom_call", output_to_operand_aliasing={{}: (6, {})} | custom-call | flops 1879048192 | bytes 3670016 | tf_op jit(solution)/shard_map/update_rows/pallas_call | solution.py:421
  90.9 0.0 collective-permute-done.b_ref
  90.9 0.0 collective-permute-done.2.code_ref
  90.9 0.0 copy-done
  90.9 1.2 %add_decode.1 = bf16[1024,512]{1,0:T(8,128)(2,1)} custom-call(f32[1024,512]{1,0:T(8,128)S(1)} %copy-done, f32[1024,512]{1,0:T(8,128)S(1)} %collective-permute-done.b_ref, s16[1056,512]{1,0:T(8,128)(2,1)S(1)} %collective-permute-done.2.code_ref), custom_call_target="tpu_custom_call" | custom-call | flops 4194304 | bytes 6291456 | tf_op jit(solution)/shard_map/add_decode/pallas_call | solution.py:316
  (4 shorter events, 0.1 us)
Async XLA Ops:
  0.6 26.5 %collective-permute-start.3 = (bf16[1024,512]{1,0:T(8,128)(2,1)}, bf16[1024,512]{1,0:T(8,128)(2,1)}, u32[]{:S(2)}, u32[]{:S(2)}) collective-permute-start(bf16[1024,512]{1,0:T(8,128)(2,1)} %refs_2_.1), channel_id=1, source_target_pairs={{0,2},{1,3},{2,0},{3,1},{4,6},{5,7},{6,4},{7,5},{8,10},{9,11},{10,... | collective-permute-start | bytes 3145736 | tf_op jit(solution)/shard_map/ppermute | solution.py:449
  3.7 8.0 %copy-start.2 = (bf16[1024,512]{1,0:T(8,128)(2,1)S(1)}, bf16[1024,512]{1,0:T(8,128)(2,1)}, u32[]{:S(2)}) copy-start(bf16[1024,512]{1,0:T(8,128)(2,1)} %refs_2_.1) | copy-start | bytes 3145732
  11.6 23.9 %copy-start.3 = (s32[8,32,28]{1,0,2:T(8,128)S(1)}, s32[8,32,28]{1,0,2:T(8,128)}, u32[]{:S(2)}) copy-start(s32[8,32,28]{1,0,2:T(8,128)} %param.17) | copy-start | bytes 86020
  11.6 24.0 %copy-start.5 = (f32[64,64]{1,0:T(8,128)S(1)}, f32[64,64]{1,0:T(8,128)}, u32[]{:S(2)}) copy-start(f32[64,64]{1,0:T(8,128)} %constant.23.clone.refs_6_) | copy-start | bytes 49156
  11.6 39.4 %collective-permute-start.1 = (f32[1024,512]{1,0:T(8,128)}, f32[1024,512]{1,0:T(8,128)}, u32[]{:S(2)}, u32[]{:S(2)}) collective-permute-start(f32[1024,512]{1,0:T(8,128)} %get-tuple-element.14), channel_id=1, source_target_pairs={{0,1},{1,0},{2,3},{3,2},{4,5},{5,4},{6,7},{7,6},{8,9},{9,8},{10,11... | collective-permute-start | bytes 6291464 | tf_op jit(solution)/shard_map/ppermute | solution.py:449
  11.7 23.9 %collective-permute-start.5 = (bf16[1024,512]{1,0:T(8,128)(2,1)S(1)}, bf16[1024,512]{1,0:T(8,128)(2,1)}, u32[]{:S(2)}, u32[]{:S(2)}) collective-permute-start(bf16[1024,512]{1,0:T(8,128)(2,1)S(1)} %copy-done.2), channel_id=1, source_target_pairs={{0,1},{1,0},{2,3},{3,2},{4,5},{5,4},{6,7},{7,6},{8,9},{9,8},{10,11... | collective-permute-start | bytes 3145736 | tf_op jit(solution)/shard_map/ppermute | solution.py:449
  27.1 26.6 %collective-permute-start.4 = (bf16[1024,512]{1,0:T(8,128)(2,1)}, bf16[1024,512]{1,0:T(8,128)(2,1)}, u32[]{:S(2)}, u32[]{:S(2)}) collective-permute-start(bf16[1024,512]{1,0:T(8,128)(2,1)} %collective-permute-done.3.refs_2_), channel_id=1, source_target_pairs={{0,1},{1,0},{2,3},{3,2},{4,5},{5,4},{6,7},{7,6},{8,9},{9,8},{10,11... | collective-permute-start | bytes 3145736 | tf_op jit(solution)/shard_map/ppermute | solution.py:449
  35.0 55.9 %collective-permute-start = (f32[1024,512]{1,0:T(8,128)}, f32[1024,512]{1,0:T(8,128)S(1)}, u32[]{:S(2)}, u32[]{:S(2)}) collective-permute-start(f32[1024,512]{1,0:T(8,128)} %get-tuple-element.12), channel_id=1, source_target_pairs={{0,1},{1,0},{2,3},{3,2},{4,5},{5,4},{6,7},{7,6},{8,9},{9,8},{10,11... | collective-permute-start | bytes 6291464 | tf_op jit(solution)/shard_map/ppermute | solution.py:449
  35.6 16.0 %copy-start.1 = (f32[1024,512]{1,0:T(8,128)S(1)}, f32[1024,512]{1,0:T(8,128)}, u32[]{:S(2)}) copy-start(f32[1024,512]{1,0:T(8,128)} %get-tuple-element.13.a_ref) | copy-start | bytes 6291460
  47.0 19.9 %collective-permute-start.12 = (s16[16,1920]{1,0:T(8,128)(2,1)S(1)}, s16[16,1920]{1,0:T(8,128)(2,1)S(1)}, u32[]{:S(2)}, u32[]{:S(2)}) collective-permute-start(s16[16,1920]{1,0:T(8,128)(2,1)S(1)} %get-tuple-element.18), channel_id=1, source_target_pairs={{0,24},{4,28},{8,16},{12,20},{16,8},{20,12},{24,0},{28,4},{1,25},{... | collective-permute-start | bytes 184328 | tf_op jit(solution)/shard_map/ppermute | solution.py:449
  51.0 19.6 %collective-permute-start.11 = (s16[16,1920]{1,0:T(8,128)(2,1)S(1)}, s16[16,1920]{1,0:T(8,128)(2,1)S(1)}, u32[]{:S(2)}, u32[]{:S(2)}) collective-permute-start(s16[16,1920]{1,0:T(8,128)(2,1)S(1)} %get-tuple-element.18), channel_id=1, source_target_pairs={{0,16},{4,20},{8,24},{12,28},{16,0},{20,4},{24,8},{28,12},{1,17},{... | collective-permute-start | bytes 184328 | tf_op jit(solution)/shard_map/ppermute | solution.py:449
  51.0 19.6 %collective-permute-start.10 = (s16[16,1920]{1,0:T(8,128)(2,1)S(1)}, s16[16,1920]{1,0:T(8,128)(2,1)S(1)}, u32[]{:S(2)}, u32[]{:S(2)}) collective-permute-start(s16[16,1920]{1,0:T(8,128)(2,1)S(1)} %get-tuple-element.18), channel_id=1, source_target_pairs={{0,8},{4,12},{8,0},{12,4},{16,24},{20,28},{24,16},{28,20},{1,9},{5... | collective-permute-start | bytes 184328 | tf_op jit(solution)/shard_map/ppermute | solution.py:449
  53.7 37.2 %collective-permute-start.2 = (s16[1056,512]{1,0:T(8,128)(2,1)S(1)}, s16[1056,512]{1,0:T(8,128)(2,1)S(1)}, u32[]{:S(2)}, u32[]{:S(2)}) collective-permute-start(s16[1056,512]{1,0:T(8,128)(2,1)S(1)} %add_encode.1), channel_id=1, source_target_pairs={{0,2},{1,3},{2,0},{3,1},{4,6},{5,7},{6,4},{7,5},{8,10},{9,11},{10,... | collective-permute-start | bytes 3244040 | tf_op jit(solution)/shard_map/ppermute | solution.py:449
  55.4 26.3 %copy-start.4 = (bf16[64,192]{1,0:T(8,128)(2,1)S(1)}, bf16[64,192]{1,0:T(8,128)(2,1)}, u32[]{:S(2)}) copy-start(bf16[64,192]{1,0:T(8,128)(2,1)} %constant.28.ct_ref) | copy-start | bytes 73732
  66.9 6.2 %collective-permute-start.8 = (s16[16,1920]{1,0:T(8,128)(2,1)S(1)}, s16[16,1920]{1,0:T(8,128)(2,1)S(1)}, u32[]{:S(2)}, u32[]{:S(2)}) collective-permute-start(s16[16,1920]{1,0:T(8,128)(2,1)S(1)} %get-tuple-element.17), channel_id=1, source_target_pairs={{0,24},{4,28},{8,16},{12,20},{16,8},{20,12},{24,0},{28,4},{1,25},{... | collective-permute-start | bytes 184328 | tf_op jit(solution)/shard_map/ppermute | solution.py:449
  70.6 5.1 %collective-permute-start.7 = (s16[16,1920]{1,0:T(8,128)(2,1)S(1)}, s16[16,1920]{1,0:T(8,128)(2,1)S(1)}, u32[]{:S(2)}, u32[]{:S(2)}) collective-permute-start(s16[16,1920]{1,0:T(8,128)(2,1)S(1)} %get-tuple-element.17), channel_id=1, source_target_pairs={{0,16},{4,20},{8,24},{12,28},{16,0},{20,4},{24,8},{28,12},{1,17},{... | collective-permute-start | bytes 184328 | tf_op jit(solution)/shard_map/ppermute | solution.py:449
  70.6 5.1 %collective-permute-start.6 = (s16[16,1920]{1,0:T(8,128)(2,1)S(1)}, s16[16,1920]{1,0:T(8,128)(2,1)S(1)}, u32[]{:S(2)}, u32[]{:S(2)}) collective-permute-start(s16[16,1920]{1,0:T(8,128)(2,1)S(1)} %get-tuple-element.17), channel_id=1, source_target_pairs={{0,8},{4,12},{8,0},{12,4},{16,24},{20,28},{24,16},{28,20},{1,9},{5... | collective-permute-start | bytes 184328 | tf_op jit(solution)/shard_map/ppermute | solution.py:449
  73.1 8.6 %collective-permute-start.13 = (s16[4,16,1920]{2,1,0:T(8,128)(2,1)S(1)}, s16[4,16,1920]{2,1,0:T(8,128)(2,1)S(1)}, u32[]{:S(2)}, u32[]{:S(2)}) collective-permute-start(s16[4,16,1920]{2,1,0:T(8,128)(2,1)S(1)} %pad_add_fusion.1.near_ref), channel_id=1, source_target_pairs={{0,4},{4,0},{8,12},{12,8},{16,20},{20,16},{24,28},{28,24},{1,5},{5... | collective-permute-start | bytes 737288 | tf_op jit(solution)/shard_map/ppermute | solution.py:449
  75.7 10.6 %collective-permute-start.9 = (s16[4,16,1920]{2,1,0:T(8,128)(2,1)S(1)}, s16[4,16,1920]{2,1,0:T(8,128)(2,1)S(1)}, u32[]{:S(2)}, u32[]{:S(2)}) collective-permute-start(s16[4,16,1920]{2,1,0:T(8,128)(2,1)S(1)} %pad_add_fusion.near_ref), channel_id=1, source_target_pairs={{0,4},{4,0},{8,12},{12,8},{16,20},{20,16},{24,28},{28,24},{1,5},{5... | collective-permute-start | bytes 737288 | tf_op jit(solution)/shard_map/ppermute | solution.py:449
  86.3 4.6 %copy-start = (f32[1024,512]{1,0:T(8,128)S(1)}, f32[1024,512]{1,0:T(8,128)}, u32[]{:S(2)}) copy-start(f32[1024,512]{1,0:T(8,128)} %get-tuple-element.11.a_ref) | copy-start | bytes 6291460
